TPU v7x, 128 devices: a whole 4x4x4 slice. The times are simulated.
128 devices in a mesh: node: 128 (over y, z, x, core).
Axes of the slice: x: 4, y: 4, z: 4, core: 2. Of those that a mesh axis runs over, the one named last changes fastest.
Arguments:
- node_feats: bfloat16 [131072, 128], P('node'), may hold values from -240 to 240
- weight: bfloat16 [128, 128], replicated, may hold values from -0.5 to 0.5
- att_src: float32 [8, 16], replicated, may hold values from -1.5 to 1.5
- att_dst: float32 [8, 16], replicated, may hold values from -1.5 to 1.5
- out_bias: float32 [128], replicated, may hold values from -3 to 3
- requests: int32 [128, 128], P('node'), may hold values from 0 to 7
- tile_dst: int32 [128, 128], P('node'), may hold values from 0 to 7, as said below
- tile_src: int32 [128, 128], P('node'), may hold values from 0 to 127
- tile_masks: int32 [128, 128, 128, 128], P('node'), may hold values from 0 to 1
- tile_count: int32 [128], P('node'), may hold values from 16 to 128, as said below
Outputs:
- node_out: bfloat16 [131072, 128], P('node')
Inputs may be any that keep to these rules, and one draw needn't show every extreme that they name: Within one device the pairs (tile_dst, tile_src) of its 128 slots are distinct. `tile_count`: slots at or past a device's count are unused; some device uses all 128.
All inputs are finite; a program needn't handle non-finite values.
Results may differ from a plain program's by a relative error of at most 0.012.
Values may be sent and summed in bfloat16 or wider, within the bound.
A program may use at most 128 MiB of HBM per device.

v0:
```python
import functools

import jax
import jax.numpy as jnp
from jax import lax
from jax.experimental import pallas as pl
from jax.experimental.pallas import tpu as pltpu
from jax.sharding import PartitionSpec as P

HEADS = 8
HD = 16
F = 128
BLK = 128
NB = 8
TILES = 128
PEERS = 128
CHUNK = 8
BF = jnp.bfloat16
F32 = jnp.float32
LOW = 40.0
HIGH = 30.0
NT = (((1,), (1,)), ((), ()))


def leaky(v):
    return jnp.maximum(v, 0.2 * v)


def nt_dot(a, b):
    return lax.dot_general(a, b, NT, preferred_element_type=F32)


def split3(a):
    hi = a.astype(BF)
    r1 = a - hi.astype(F32)
    mid = r1.astype(BF)
    lo = (r1 - mid.astype(F32)).astype(BF)
    return hi, mid, lo


def nt_exact(a, b):
    hi, mid, lo = split3(b)
    return (nt_dot(a, lo) + nt_dot(a, mid)) + nt_dot(a, hi)


def iota(shape, dim):
    return lax.broadcasted_iota(jnp.int32, shape, dim)


def attend_kernel(dst_ref, src_ref, cnt_ref, own_ref, far_ref, atts_ref, attd_ref, bias_ref, mask_hbm,
                  out_ref, masks, q_ref, b_ref, d_ref, s_ref, acc, dmat, pmat, slog, sem):
    nchunk = TILES // CHUNK

    def mask_copy(c):
        rows = pl.ds(c * CHUNK, CHUNK)
        return pltpu.make_async_copy(mask_hbm.at[rows], masks.at[rows], sem.at[c])

    def start(c, _):
        mask_copy(c).start()
        return 0

    lax.fori_loop(0, nchunk, start, 0)

    head_of_lane = iota((HEADS, F), 1) // HD
    row_head = iota((HEADS, F), 0)
    own_head = head_of_lane == row_head

    def spread(att):
        return jnp.where(own_head, jnp.concatenate([att] * HEADS, axis=1), 0.0)

    a_s = spread(atts_ref[...])
    a_d = spread(attd_ref[...])
    hi, mid, lo = split3(a_s)
    a24 = jnp.concatenate([hi.astype(F32), mid.astype(F32), lo.astype(F32)], axis=0).astype(BF)

    def score_rows(blocks):
        r = nt_dot(a24, blocks)
        return (r[16:24] + r[8:16]) + r[0:8]

    own_s = score_rows(own_ref[...])
    sig_col = jnp.max(own_s, axis=1, keepdims=True)
    sig_x = jnp.sum(jnp.where(own_head, sig_col, 0.0), axis=0, keepdims=True)

    square_head = iota((F, F), 0) // HD
    same_head = square_head == iota((F, F), 1) // HD
    flat_s = jnp.sum(a_s, axis=0, keepdims=True)
    flat_d = jnp.sum(a_d, axis=0, keepdims=True)
    own = own_ref[...]
    sx = nt_exact(own, jnp.where(same_head, flat_s, 0.0))
    dx = nt_exact(own, jnp.where(same_head, flat_d, 0.0))

    lane = iota((NB * BLK, F), 1)
    first_half = lane < F // 2

    qx = jnp.exp(0.8 * jnp.minimum(dx + sig_x, LOW)).astype(BF)
    for h in range(HEADS):
        pick = (iota((F, F), 0) == h * HD).astype(F32).astype(BF)
        col = jnp.dot(qx, pick, preferred_element_type=F32)
        q_ref[:, h] = col.astype(BF).reshape(NB, BLK, F)

    def init_acc(w):
        vals = own_ref[...].astype(F32)
        turned = pltpu.roll(w, F // 2, 1)
        wv = w * vals
        acc[:, :, 0:F] = jnp.where(first_half, wv, turned).reshape(NB, BLK, F)
        acc[:, :, F:2 * F] = jnp.where(first_half, turned, wv).reshape(NB, BLK, F)

    xo = sx - sig_x
    init_acc(jnp.maximum(qx.astype(F32) * jnp.exp(xo), jnp.exp(0.2 * xo)))

    pair = 2

    def far_scores(i, carry):
        low, high = carry
        p = i * pair
        two = far_ref[pl.ds(p, pair)].reshape(pair * BLK, F)
        raw = score_rows(two)
        s = raw - sig_col
        for k in range(pair):
            part = s[:, k * BLK:(k + 1) * BLK]
            s_ref[p + k] = raw[:, k * BLK:(k + 1) * BLK]
            b_ref[p + k] = jnp.exp(part)
            d_ref[p + k] = jnp.exp(0.2 * part)
            low = jnp.minimum(low, part)
            high = jnp.maximum(high, part)
        return low, high

    zero = jnp.zeros((HEADS, BLK), F32)
    low, high = lax.fori_loop(0, PEERS // pair, far_scores, (zero, zero), unroll=8)
    low = jnp.minimum(low, jnp.min(own_s - sig_col, axis=1, keepdims=True))
    bounded = jnp.logical_and(jnp.min(low) >= -LOW, jnp.max(high) <= HIGH)
    count = cnt_ref[0]

    lane1 = iota((BLK, F), 1)

    def values(src):
        v = far_ref[src]
        sides = []
        for half in range(2):
            parts = []
            for k in range(HEADS // 2):
                h = half * (HEADS // 2) + k
                mine = lane1 // HD == h
                ones = lane1 // HD == (h + HEADS // 2) % HEADS
                parts.append(jnp.where(mine, v, jnp.where(ones, 1.0, 0.0).astype(BF)))
            sides.append(jnp.concatenate(parts, axis=0))
        return sides

    def add_tile(dst, src, weight_of):
        sides = values(src)
        for half in range(2):
            w = jnp.concatenate([weight_of(half * (HEADS // 2) + k) for k in range(HEADS // 2)], axis=1)
            o = jnp.dot(w, sides[half], preferred_element_type=F32)
            acc[dst, :, half * F:(half + 1) * F] += o

    @pl.when(bounded)
    def _():
        def chunk(c, _):
            mask_copy(c).wait()
            live = jnp.clip(count - c * CHUNK, 0, CHUNK)

            def tile(k, _):
                t = c * CHUNK + k
                dst = dst_ref[t]
                src = src_ref[t]
                m = masks[t].astype(F32).astype(BF).reshape(BLK // 16, 16, BLK)

                def weight_of(h):
                    bj = jnp.broadcast_to(b_ref[src, h:h + 1, :], (16, BLK)).astype(BF)
                    dj = jnp.broadcast_to(d_ref[src, h:h + 1, :], (16, BLK)).astype(BF)
                    q = q_ref[dst, h].reshape(BLK // 16, 16, BLK)
                    return (m * jnp.maximum(q * bj[None], dj[None])).reshape(BLK, BLK)

                add_tile(dst, src, weight_of)
                return 0

            lax.fori_loop(0, live, tile, 0)
            return 0

        lax.fori_loop(0, nchunk, chunk, 0)

    @pl.when(jnp.logical_not(bounded))
    def _():
        def finish(c, _):
            mask_copy(c).wait()
            return 0

        lax.fori_loop(0, nchunk, finish, 0)

        for h in range(HEADS):
            dh = jnp.broadcast_to(a_d[h:h + 1], (F, F))
            sh = jnp.broadcast_to(a_s[h:h + 1], (F, F))

            def rows(b, _):
                ob = own_ref[pl.ds(b * BLK, BLK)]
                d = nt_exact(ob, dh)
                dmat[b, h] = d
                pmat[b, h] = leaky(d + nt_exact(ob, sh))
                return 0

            lax.fori_loop(0, NB, rows, 0)

        def expand(b):
            px = pmat[b, 0]
            for h in range(1, HEADS):
                px = jnp.where(lane1 // HD == h, pmat[b, h], px)
            return px

        def keep(b, _):
            slog[pl.ds(b * BLK, BLK)] = expand(b)
            return 0

        lax.fori_loop(0, NB, keep, 0)

        def peak(t, _):
            dst = dst_ref[t]
            src = src_ref[t]
            edge = masks[t] > 0
            for h in range(HEADS):
                lg = leaky(dmat[dst, h] + s_ref[src, h:h + 1, :])
                top = jnp.max(jnp.where(edge, lg, -jnp.inf), axis=1, keepdims=True)
                pmat[dst, h] = jnp.maximum(pmat[dst, h], top)
            return 0

        lax.fori_loop(0, count, peak, 0)

        def settle(b, _):
            rows = pl.ds(b * BLK, BLK)
            slog[rows] = jnp.exp(slog[rows] - expand(b))
            return 0

        lax.fori_loop(0, NB, settle, 0)
        init_acc(slog[...])

        def tile(t, _):
            dst = dst_ref[t]
            src = src_ref[t]
            edge = masks[t] > 0

            def weight_of(h):
                lg = leaky(dmat[dst, h] + s_ref[src, h:h + 1, :])
                return jnp.exp(jnp.where(edge, lg - pmat[dst, h], -jnp.inf)).astype(BF)

            add_tile(dst, src, weight_of)
            return 0

        lax.fori_loop(0, count, tile, 0)

    bias = bias_ref[...]
    for b in range(NB):
        one = acc[b, :, 0:F]
        two = acc[b, :, F:2 * F]
        left = lane1 < F // 2
        top = jnp.where(left, one, two)
        low_part = pltpu.roll(jnp.where(left, two, one), F // 2, 1)
        mixed = top / low_part + bias
        small = mixed * (1.0 + mixed * (0.5 + mixed * (1.0 / 6.0 + mixed * (1.0 / 24.0))))
        neg = jnp.where(mixed > -0.0625, small, jnp.exp(jnp.minimum(mixed, 0.0)) - 1.0)
        out_ref[pl.ds(b * BLK, BLK)] = jnp.where(mixed > 0, mixed, neg).astype(BF)


def attend(own, far, att_src, att_dst, out_bias, dst, src, masks, count):
    vm = pl.BlockSpec(memory_space=pltpu.VMEM)
    sm = pl.BlockSpec(memory_space=pltpu.SMEM)
    return pl.pallas_call(
        attend_kernel,
        out_shape=jax.ShapeDtypeStruct((NB * BLK, F), BF),
        in_specs=[sm, sm, sm, vm, vm, vm, vm, vm, pl.BlockSpec(memory_space=pl.ANY)],
        out_specs=vm,
        scratch_shapes=[
            pltpu.VMEM((TILES, BLK, BLK), jnp.int32),
            pltpu.VMEM((NB, HEADS, BLK, F), BF),
            pltpu.VMEM((PEERS, HEADS, BLK), F32),
            pltpu.VMEM((PEERS, HEADS, BLK), F32),
            pltpu.VMEM((PEERS, HEADS, BLK), F32),
            pltpu.VMEM((NB, BLK, 2 * F), F32),
            pltpu.VMEM((NB, HEADS, BLK, F), F32),
            pltpu.VMEM((NB, HEADS, BLK, F), F32),
            pltpu.VMEM((NB * BLK, F), F32),
            pltpu.SemaphoreType.DMA((TILES // CHUNK,)),
        ],
        compiler_params=pltpu.CompilerParams(vmem_limit_bytes=52 * 1024 * 1024),
        name="attend",
    )(dst, src, count, own, far, att_src, att_dst, out_bias.reshape(1, F), masks)


SIDE = 4
SPLIT = (("z", "y", "x", 0, 48), ("x", "z", "y", 48, 48), ("y", "x", "z", 96, 32))
AXES = ("y", "z", "x")
OTHERS = tuple((off, flip) for off in (1, 3, 2) for flip in (0, 1))
LINE = ((0, 1),) + OTHERS


def peer_list():
    peers = [("x", 0, 1)]
    for axis in AXES:
        for off, flip in OTHERS:
            peers.append((axis, off, flip))
    return peers


PEER_LIST = peer_list()


def peer_slot(axis, off, flip):
    if off == 0:
        return 0
    return PEER_LIST.index((axis, off, flip))


def place(pos, core):
    return ((pos["y"] * SIDE + pos["z"]) * SIDE + pos["x"]) * 2 + core


def exchange_kernel(x_ref, w_ref, req_ref, req_s, far_ref, own_ref, *scratch):
    gathered = tuple(scratch[SIDE * c:SIDE * c + SIDE] for c in range(3))
    picked = scratch[3 * SIDE:3 * SIDE + 3]
    (rq, rqs, ask_s, ask_r, one_s, one_r, two_s, two_r, out_s, out_r, local_sem, smem_sem) = scratch[3 * SIDE + 3:]
    me = lax.axis_index("node")
    core = lax.rem(me, 2)
    pos = {
        "x": lax.rem(lax.div(me, 2), SIDE),
        "z": lax.rem(lax.div(me, 2 * SIDE), SIDE),
        "y": lax.div(me, 2 * SIDE * SIDE),
    }

    def shifted(axis, off):
        return lax.rem(pos[axis] + off, SIDE)

    def device(axis, off, flip):
        where = dict(pos)
        where[axis] = shifted(axis, off)
        return place(where, lax.rem(core + flip, 2))

    def send(src, dst, ssem, rsem, axis, off, flip):
        return pltpu.make_async_remote_copy(
            src_ref=src, dst_ref=dst, send_sem=ssem, recv_sem=rsem,
            device_id=(device(axis, off, flip),), device_id_type=pl.DeviceIdType.MESH,
        )

    barrier = pltpu.get_barrier_semaphore()
    for axis, off, flip in PEER_LIST:
        pl.semaphore_signal(barrier, inc=1, device_id=(device(axis, off, flip),), device_id_type=pl.DeviceIdType.MESH)

    proj = jnp.dot(x_ref[...], w_ref[...], preferred_element_type=F32).astype(BF)
    own_ref[...] = proj
    blocks = proj.reshape(NB, BLK, F)
    for c, (ga, gb, gf, row, rows) in enumerate(SPLIT):
        gathered[c][0][pos[ga]] = blocks[:, row:row + rows]

    pl.semaphore_wait(barrier, len(PEER_LIST))

    def ask(i, back=False):
        axis, off, flip = PEER_LIST[i]
        return send(req_ref, rq.at[i], ask_s.at[i], ask_r.at[i], axis, off, flip)

    steps = (1, 3, 2)

    def first(c, i, back=False):
        ga = SPLIT[c][0]
        off = steps[i]
        mine = gathered[c][0].at[pos[ga]]
        dst = gathered[c][0].at[shifted(ga, SIDE - off)] if back else mine
        return send(mine, dst, one_s.at[c, i], one_r.at[c, i], ga, off, 0)

    turns = (0, 1, 3, 2)

    def second(c, q, i):
        ga, gb = SPLIT[c][:2]
        off = steps[i]
        at = shifted(ga, (SIDE - turns[q]) % SIDE)
        src = gathered[c][0].at[at]
        return send(src, gathered[c][i + 1].at[at], two_s.at[c, q, i], two_r.at[c, q, i], gb, off, 0)

    def landing(c, b_at, f_at, from_core):
        ga, gb, gf, row, rows = SPLIT[c]
        spot = {ga: pl.ds(0, SIDE), gb: b_at, gf: f_at}
        return far_ref.at[spot["y"], spot["z"], spot["x"], from_core, pl.ds(row, rows)]

    def third(c, q, j, back=False):
        ga, gb, gf, row, rows = SPLIT[c]
        off, flip = LINE[j]
        b_at = shifted(gb, (SIDE - turns[q]) % SIDE)
        src = picked[c].at[q, j]
        if back:
            dst = landing(c, b_at, shifted(gf, (SIDE - off) % SIDE), lax.rem(core + flip, 2))
        else:
            dst = landing(c, b_at, pos[gf], core)
        return send(src, dst, out_s.at[c, q, j], out_r.at[c, q, j], gf, off, flip)

    def stay(c, q):
        gb, gf = SPLIT[c][1:3]
        b_at = shifted(gb, (SIDE - turns[q]) % SIDE)
        return pltpu.make_async_copy(picked[c].at[q, len(LINE)], landing(c, b_at, pos[gf], core), local_sem.at[c, q])

    for c in range(3):
        for i in range(3):
            first(c, i).start()
    for i in range(len(PEER_LIST)):
        ask(i).start()
    for i in range(3):
        for c in range(3):
            second(c, 0, i).start()
    for q in range(1, SIDE):
        for c in range(3):
            first(c, q - 1, True).wait_recv()
            for i in range(3):
                second(c, q, i).start()
    for i in range(len(PEER_LIST)):
        ask(i).wait_recv()
    fetch = pltpu.make_async_copy(rq, rqs, smem_sem.at[0])
    fetch.start()
    fetch.wait()

    def pick(c, q):
        ga, gb, gf, row, rows = SPLIT[c]
        b_at = shifted(gb, (SIDE - turns[q]) % SIDE)
        for j in range(len(LINE) + 1):
            for a_at in range(SIDE):
                where = {ga: a_at, gb: b_at, gf: pos[gf]}
                col = place(where, core)
                if j < len(LINE):
                    off, flip = LINE[j]
                    block = rqs[peer_slot(gf, (SIDE - off) % SIDE, flip), 0, col]
                else:
                    block = req_s[0, col]
                picked[c][q, j, a_at] = gathered[c][q][a_at, block]

    for q in range(SIDE):
        for c in range(3):
            if q:
                for k in range(SIDE):
                    second(c, k, q - 1).wait_recv()
            pick(c, q)
            for j in range(len(LINE)):
                third(c, q, j).start()
            stay(c, q).start()

    for q in range(SIDE):
        for c in range(3):
            for j in range(len(LINE)):
                third(c, q, j, True).wait_recv()
            stay(c, q).wait()
    for i in range(len(PEER_LIST)):
        ask(i).wait_send()
    for c in range(3):
        for i in range(3):
            first(c, i).wait_send()
        for q in range(SIDE):
            for i in range(3):
                second(c, q, i).wait_send()
            for j in range(len(LINE)):
                third(c, q, j).wait_send()


def exchange(x, weight, requests):
    vm = pl.BlockSpec(memory_space=pltpu.VMEM)
    dma = pltpu.SemaphoreType.DMA
    peers = len(PEER_LIST)
    lines = len(LINE)
    return pl.pallas_call(
        exchange_kernel,
        out_shape=(
            jax.ShapeDtypeStruct((SIDE, SIDE, SIDE, 2, BLK, F), BF),
            jax.ShapeDtypeStruct((NB * BLK, F), BF),
        ),
        in_specs=[vm, vm, vm, pl.BlockSpec(memory_space=pltpu.SMEM)],
        out_specs=(pl.BlockSpec(memory_space=pl.ANY), vm),
        scratch_shapes=(
            [pltpu.VMEM((SIDE, NB, rows, F), BF) for *_, rows in SPLIT for _ in range(SIDE)]
            + [pltpu.VMEM((SIDE, lines + 1, SIDE, rows, F), BF) for *_, rows in SPLIT]
            + [
                pltpu.VMEM((peers, 1, PEERS), jnp.int32),
                pltpu.SMEM((peers, 1, PEERS), jnp.int32),
                dma((peers,)), dma((peers,)),
                dma((3, 3)), dma((3, 3)),
                dma((3, SIDE, 3)), dma((3, SIDE, 3)),
                dma((3, SIDE, lines)), dma((3, SIDE, lines)),
                dma((3, SIDE)), dma((1,)),
            ]
        ),
        compiler_params=pltpu.CompilerParams(
            collective_id=0, has_side_effects=True, vmem_limit_bytes=32 * 1024 * 1024
        ),
        name="exchange",
    )(x, weight, requests, requests)


def local(node_feats, weight, att_src, att_dst, out_bias, requests, tile_dst, tile_src, tile_masks, tile_count):
    far, own = exchange(node_feats, weight, requests)
    far = far.reshape(PEERS, BLK, F)
    return attend(own, far, att_src, att_dst, out_bias, tile_dst[0], tile_src[0], tile_masks[0], tile_count)


def solution(mesh):
    placed = (
        P("node", None), P(), P(), P(), P(), P("node", None), P("node", None), P("node", None),
        P("node", None, None, None), P("node"),
    )
    return jax.shard_map(local, mesh=mesh, in_specs=placed, out_specs=P("node", None), check_vma=False)
```

profile of v0, /device:TPU:0, one launch (start us, length us, event | category | flops | bytes accessed | tf_op | source)
XLA Modules:
  0.0 147.2 jit_solution(13531361390380668416)
XLA Ops:
  0.7 0.0 copy-start.1
  0.7 0.9 copy-done.1
  1.6 0.0 copy-start.2
  1.6 0.8 copy-done.2
  2.4 0.0 copy-start.5
  2.4 0.7 copy-done.5
  3.0 48.3 %exchange.1 = (bf16[4,4,4,2,128,128]{5,4,3,2,1,0:T(8,128)(2,1)S(1)}, bf16[1024,128]{1,0:T(8,128)(2,1)S(1)}) custom-call(bf16[1024,128]{1,0:T(8,128)(2,1)S(1)} %copy-done.1, bf16[128,128]{1,0:T(8,128)(2,1)S(1)} %copy-done.2, s32[1,128]{1,0:T(1,128)S(1)} %copy-done.5, s32[1,128]{1,0:T(1,128)S(1)} %copy-done.5), custom_call_target="tpu_custom_call" | custom-call | tf_op jit(solution)/shard_map/exchange/pallas_call | solution.py:461
  51.3 0.0 copy-start
  51.3 1.9 %copy-done = bf16[4,4,4,2,128,128]{5,4,3,2,1,0:T(8,128)(2,1)} copy-done((bf16[4,4,4,2,128,128]{5,4,3,2,1,0:T(8,128)(2,1)}, bf16[4,4,4,2,128,128]{5,4,3,2,1,0:T(8,128)(2,1)S(1)}, u32[]{:S(2)}) %copy-start) | copy-done | bytes 4194328
  53.2 0.0 copy-start.3
  53.2 0.7 copy-done.3
  53.9 0.0 copy-start.4
  53.9 0.7 copy-done.4
  54.6 0.0 copy-start.6
  54.6 0.7 copy-done.6
  55.3 0.0 copy-start.7
  55.3 0.7 copy-done.7
  55.9 0.0 copy-start.8
  55.9 0.7 copy-done.8
  56.6 90.6 %attend.1 = bf16[1024,128]{1,0:T(8,128)(2,1)} custom-call(s32[128]{0:T(128)S(1)} %bitcast.6, s32[128]{0:T(128)S(1)} %bitcast.7, s32[1]{0:T(128)S(6)} %copy.11.cnt_ref, bf16[1024,128]{1,0:T(8,128)(2,1)S(1)} %get-tuple-element.7.own_ref, bf16[128,128,128]{2,1,0:T(8,128)(2,1)} %bitcast.5, f32[8,16]{1,0:T(8,128)S(1)} %copy-done.3, f32[8,16]{1,0:T(8,128)S(1)} %copy-done.4, ...), custom_call_target="tpu_custom_call" | custom-call | tf_op jit(solution)/shard_map/attend/pallas_call | solution.py:265
Async XLA Ops:
  0.7 1.0 copy-start.1
  1.6 0.8 copy-start.2
  2.4 0.7 copy-start.5
  51.3 1.9 %copy-start = (bf16[4,4,4,2,128,128]{5,4,3,2,1,0:T(8,128)(2,1)}, bf16[4,4,4,2,128,128]{5,4,3,2,1,0:T(8,128)(2,1)S(1)}, u32[]{:S(2)}) copy-start(bf16[4,4,4,2,128,128]{5,4,3,2,1,0:T(8,128)(2,1)S(1)} %get-tuple-element.8) | copy-start | bytes 12582916
  53.2 0.7 copy-start.3
  53.9 0.7 copy-start.4
  54.6 0.7 copy-start.6
  55.3 0.7 copy-start.7
  55.9 0.7 copy-start.8
where the time goes:
time: 148 us; the launch traced here: 147 us
  Pallas kernels  139 us (94%)
  local copies, waits for them, and re-layouts  7.63 us (5%)
    pallas_call x1, Pallas kernels, attend(): pl.pallas_call(attend_kernel, out_shape=jax.ShapeDtypeStruct((NB * BLK, F...  90.6 us
    pallas_call x1, Pallas kernels, exchange(): pl.pallas_call(exchange_kernel, out_shape=(jax.ShapeDtypeStruct((SIDE, SI...  48.3 us
    unnamed x18, local copies, waits for them, and re-layouts  7.63 us

commit v1 on v0

--- a/solution.py
+++ b/solution.py
@@ -15,6 +15,8 @@
 TILES = 128
 PEERS = 128
 CHUNK = 8
+GROUP = 4
+ROWS = 16
 BF = jnp.bfloat16
 F32 = jnp.float32
 LOW = 40.0
@@ -48,7 +50,21 @@
 
 
 def attend_kernel(dst_ref, src_ref, cnt_ref, own_ref, far_ref, atts_ref, attd_ref, bias_ref, mask_hbm,
-                  out_ref, masks, q_ref, b_ref, d_ref, s_ref, acc, dmat, pmat, slog, sem):
+                  out_ref, masks, s_ref, acc, dmat, pmat, slog, sem):
+    pl.run_scoped(
+        functools.partial(attend_body, dst_ref, src_ref, cnt_ref, own_ref, far_ref, atts_ref, attd_ref, bias_ref,
+                          mask_hbm, out_ref, masks, s_ref, acc, dmat, pmat, slog, sem),
+        pltpu.VMEM((NB, HEADS, BLK, F), BF),
+        pltpu.VMEM((PEERS, BLK, F), BF),
+        pltpu.VMEM((PEERS, HEADS, ROWS, F), BF),
+        pltpu.VMEM((PEERS, HEADS, ROWS, F), BF),
+        pltpu.VMEM((GROUP, BLK, BLK), BF),
+        pltpu.VMEM((ROWS, F), BF),
+    )
+
+
+def attend_body(dst_ref, src_ref, cnt_ref, own_ref, far_ref, atts_ref, attd_ref, bias_ref, mask_hbm,
+                out_ref, masks, s_ref, acc, dmat, pmat, slog, sem, q_ref, v_ref, b_ref, d_ref, m_ref, head_ref):
     nchunk = TILES // CHUNK
 
     def mask_copy(c):
@@ -119,8 +135,12 @@
         for k in range(pair):
             part = s[:, k * BLK:(k + 1) * BLK]
             s_ref[p + k] = raw[:, k * BLK:(k + 1) * BLK]
-            b_ref[p + k] = jnp.exp(part)
-            d_ref[p + k] = jnp.exp(0.2 * part)
+            bexp = jnp.exp(part)
+            dexp = jnp.exp(0.2 * part)
+            for h in range(HEADS):
+                b_ref[p + k, h] = jnp.broadcast_to(bexp[h:h + 1], (ROWS, BLK)).astype(BF)
+                d_ref[p + k, h] = jnp.broadcast_to(dexp[h:h + 1], (ROWS, BLK)).astype(BF)
+            v_ref[p + k] = two[k * BLK:(k + 1) * BLK]
             low = jnp.minimum(low, part)
             high = jnp.maximum(high, part)
         return low, high
@@ -132,49 +152,65 @@
     count = cnt_ref[0]
 
     lane1 = iota((BLK, F), 1)
+    head_ref[...] = (iota((ROWS, F), 1) // HD).astype(F32).astype(BF)
+    cut = (BLK // ROWS, ROWS, F)
 
     def values(src):
-        v = far_ref[src]
+        v = v_ref[src].reshape(cut)
+        head_id = head_ref[...]
         sides = []
         for half in range(2):
             parts = []
             for k in range(HEADS // 2):
                 h = half * (HEADS // 2) + k
-                mine = lane1 // HD == h
-                ones = lane1 // HD == (h + HEADS // 2) % HEADS
-                parts.append(jnp.where(mine, v, jnp.where(ones, 1.0, 0.0).astype(BF)))
+                mine = jnp.broadcast_to((head_id == h)[None], cut)
+                ones = (head_id == (h + HEADS // 2) % HEADS).astype(F32).astype(BF)
+                parts.append(jnp.where(mine, v, jnp.broadcast_to(ones[None], cut)).reshape(BLK, F))
             sides.append(jnp.concatenate(parts, axis=0))
         return sides
 
-    def add_tile(dst, src, weight_of):
+    def tile_sums(src, weight_of):
         sides = values(src)
+        sums = []
         for half in range(2):
             w = jnp.concatenate([weight_of(half * (HEADS // 2) + k) for k in range(HEADS // 2)], axis=1)
-            o = jnp.dot(w, sides[half], preferred_element_type=F32)
-            acc[dst, :, half * F:(half + 1) * F] += o
+            sums.append(jnp.dot(w, sides[half], preferred_element_type=F32))
+        return sums
+
+    def add_sums(dst, sums):
+        for half in range(2):
+            acc[dst, :, half * F:(half + 1) * F] += sums[half]
 
     @pl.when(bounded)
     def _():
         def chunk(c, _):
             mask_copy(c).wait()
-            live = jnp.clip(count - c * CHUNK, 0, CHUNK)
-
-            def tile(k, _):
-                t = c * CHUNK + k
-                dst = dst_ref[t]
-                src = src_ref[t]
-                m = masks[t].astype(F32).astype(BF).reshape(BLK // 16, 16, BLK)
-
-                def weight_of(h):
-                    bj = jnp.broadcast_to(b_ref[src, h:h + 1, :], (16, BLK)).astype(BF)
-                    dj = jnp.broadcast_to(d_ref[src, h:h + 1, :], (16, BLK)).astype(BF)
-                    q = q_ref[dst, h].reshape(BLK // 16, 16, BLK)
-                    return (m * jnp.maximum(q * bj[None], dj[None])).reshape(BLK, BLK)
-
-                add_tile(dst, src, weight_of)
+            live = jnp.clip((count - c * CHUNK + GROUP - 1) // GROUP, 0, CHUNK // GROUP)
+
+            def group(g, _):
+                todo = []
+                for k in range(GROUP):
+                    t = c * CHUNK + g * GROUP + k
+                    used = (t < count).astype(F32)
+                    m_ref[k] = (masks[t].astype(F32) * used).astype(BF)
+                for k in range(GROUP):
+                    t = c * CHUNK + g * GROUP + k
+                    dst = dst_ref[t]
+                    src = src_ref[t]
+                    m = m_ref[k].reshape(cut)
+
+                    def weight_of(h):
+                        q = q_ref[dst, h].reshape(cut)
+                        bj = jnp.broadcast_to(b_ref[src, h][None], cut)
+                        dj = jnp.broadcast_to(d_ref[src, h][None], cut)
+                        return (jnp.maximum(q * bj, dj) * m).reshape(BLK, BLK)
+
+                    todo.append((dst, tile_sums(src, weight_of)))
+                for dst, sums in todo:
+                    add_sums(dst, sums)
                 return 0
 
-            lax.fori_loop(0, live, tile, 0)
+            lax.fori_loop(0, live, group, 0)
             return 0
 
         lax.fori_loop(0, nchunk, chunk, 0)
@@ -241,7 +277,7 @@
                 lg = leaky(dmat[dst, h] + s_ref[src, h:h + 1, :])
                 return jnp.exp(jnp.where(edge, lg - pmat[dst, h], -jnp.inf)).astype(BF)
 
-            add_tile(dst, src, weight_of)
+            add_sums(dst, tile_sums(src, weight_of))
             return 0
 
         lax.fori_loop(0, count, tile, 0)
@@ -269,9 +305,6 @@
         out_specs=vm,
         scratch_shapes=[
             pltpu.VMEM((TILES, BLK, BLK), jnp.int32),
-            pltpu.VMEM((NB, HEADS, BLK, F), BF),
-            pltpu.VMEM((PEERS, HEADS, BLK), F32),
-            pltpu.VMEM((PEERS, HEADS, BLK), F32),
             pltpu.VMEM((PEERS, HEADS, BLK), F32),
             pltpu.VMEM((NB, BLK, 2 * F), F32),
             pltpu.VMEM((NB, HEADS, BLK, F), F32),
@@ -279,7 +312,7 @@
             pltpu.VMEM((NB * BLK, F), F32),
             pltpu.SemaphoreType.DMA((TILES // CHUNK,)),
         ],
-        compiler_params=pltpu.CompilerParams(vmem_limit_bytes=52 * 1024 * 1024),
+        compiler_params=pltpu.CompilerParams(vmem_limit_bytes=42 * 1024 * 1024),
         name="attend",
     )(dst, src, count, own, far, att_src, att_dst, out_bias.reshape(1, F), masks)
 

time: 148 us -> 143 us (0.966)
  the two profiles are of different devices: /device:TPU:0 before, /device:TPU:4 now
where the time goes in v1:
time: 143 us
  Pallas kernels  136 us (95%)
  local copies, waits for them, and re-layouts  5.69 us (4%)
    pallas_call x1, Pallas kernels, attend(): pl.pallas_call(attend_kernel, out_shape=jax.ShapeDtypeStruct((NB * BLK, F...  88.3 us
    pallas_call x1, Pallas kernels, exchange(): pl.pallas_call(exchange_kernel, out_shape=(jax.ShapeDtypeStruct((SIDE, SI...  47.9 us
    unnamed x16, local copies, waits for them, and re-layouts  5.69 us

profile of v1, /device:TPU:4, one launch (start us, length us, event | category | flops | bytes accessed | tf_op | source)
XLA Modules:
  0.0 142.5 jit_solution(11779144833441736417)
XLA Ops:
  0.7 0.0 copy-start
  0.7 0.9 copy-done
  1.6 0.0 copy-start.1
  1.6 0.8 copy-done.1
  2.4 0.0 copy-start.4
  2.4 0.7 copy-done.4
  3.0 47.9 %exchange.1 = (bf16[4,4,4,2,128,128]{5,4,3,2,1,0:T(8,128)(2,1)S(1)}, bf16[1024,128]{1,0:T(8,128)(2,1)S(1)}) custom-call(bf16[1024,128]{1,0:T(8,128)(2,1)S(1)} %copy-done, bf16[128,128]{1,0:T(8,128)(2,1)S(1)} %copy-done.1, s32[1,128]{1,0:T(1,128)S(1)} %copy-done.4, s32[1,128]{1,0:T(1,128)S(1)} %copy-done.4), custom_call_target="tpu_custom_call" | custom-call | tf_op jit(solution)/shard_map/exchange/pallas_call | solution.py:494
  50.9 0.0 copy-start.2
  50.9 0.7 copy-done.2
  51.6 0.0 copy-start.3
  51.6 0.7 copy-done.3
  52.3 0.0 copy-start.5
  52.3 0.7 copy-done.5
  53.0 0.0 copy-start.6
  53.0 0.7 copy-done.6
  53.6 0.0 copy-start.7
  53.6 0.7 copy-done.7
  54.3 88.3 %attend.1 = bf16[1024,128]{1,0:T(8,128)(2,1)} custom-call(s32[128]{0:T(128)S(1)} %bitcast.6, s32[128]{0:T(128)S(1)} %bitcast.7, s32[1]{0:T(128)S(6)} %copy.11.cnt_ref, bf16[1024,128]{1,0:T(8,128)(2,1)S(1)} %get-tuple-element.7.own_ref, bf16[128,128,128]{2,1,0:T(8,128)(2,1)S(1)} %bitcast.5, f32[8,16]{1,0:T(8,128)S(1)} %copy-done.2, f32[8,16]{1,0:T(8,128)S(1)} %copy-done.3, ...), custom_call_target="tpu_custom_call" | custom-call | tf_op jit(solution)/shard_map/attend/pallas_call | solution.py:301
Async XLA Ops:
  0.7 1.0 copy-start
  1.6 0.8 copy-start.1
  2.4 0.7 copy-start.4
  50.9 0.7 copy-start.2
  51.6 0.7 copy-start.3
  52.3 0.7 copy-start.5
  53.0 0.7 copy-start.6
  53.6 0.7 copy-start.7

commit v2 on v1

v2 whole, which is shorter than its diff:
```python
import functools

import jax
import jax.numpy as jnp
from jax import lax
from jax.experimental import pallas as pl
from jax.experimental.pallas import tpu as pltpu
from jax.sharding import PartitionSpec as P

HEADS = 8
HD = 16
F = 128
BLK = 128
NB = 8
TILES = 128
PEERS = 128
CHUNK = 8
GROUP = 4
PART = 16
VMEM_ALL = 67043328
ROWS = 16
BF = jnp.bfloat16
F32 = jnp.float32
LOW = 40.0
HIGH = 30.0
NT = (((1,), (1,)), ((), ()))


def leaky(v):
    return jnp.maximum(v, 0.2 * v)


def nt_dot(a, b):
    return lax.dot_general(a, b, NT, preferred_element_type=F32)


def split3(a):
    hi = a.astype(BF)
    r1 = a - hi.astype(F32)
    mid = r1.astype(BF)
    lo = (r1 - mid.astype(F32)).astype(BF)
    return hi, mid, lo


def nt_exact(a, b):
    hi, mid, lo = split3(b)
    return (nt_dot(a, lo) + nt_dot(a, mid)) + nt_dot(a, hi)


def stacked3(a):
    return jnp.concatenate([part.astype(F32) for part in split3(a)], axis=0).astype(BF)


def score_rows(a24, blocks):
    r = nt_dot(a24, blocks)
    return (r[16:24] + r[8:16]) + r[0:8]


def self_sums(acc, own, w):
    first_half = lax.broadcasted_iota(jnp.int32, (NB * BLK, F), 1) < F // 2
    turned = pltpu.roll(w, F // 2, 1)
    wv = w * own.astype(F32)
    acc[:, :, 0:F] = jnp.where(first_half, wv, turned).reshape(NB, BLK, F)
    acc[:, :, F:2 * F] = jnp.where(first_half, turned, wv).reshape(NB, BLK, F)


def iota(shape, dim):
    return lax.broadcasted_iota(jnp.int32, shape, dim)


def attend_kernel(dst_hbm, src_hbm, cnt_hbm, far_hbm, own_hbm, q_hbm, acc_hbm, par_hbm, mask_hbm,
                  out_ref, *scratch):
    pl.run_scoped(
        functools.partial(attend_body, dst_hbm, src_hbm, cnt_hbm, far_hbm, own_hbm, q_hbm, acc_hbm, par_hbm, mask_hbm,
                          out_ref, *scratch),
        pltpu.VMEM((NB, HEADS, BLK, F), BF),
        pltpu.VMEM((PEERS, BLK, F), BF),
        pltpu.VMEM((GROUP, 2, HEADS, ROWS, F), BF),
        pltpu.VMEM((GROUP, BLK, BLK), BF),
        pltpu.VMEM((ROWS, F), BF),
    )


def attend_body(dst_hbm, src_hbm, cnt_hbm, far_hbm, own_hbm, q_hbm, acc_hbm, par_hbm, mask_hbm,
                out_ref, masks, s_ref, bf_ref, df_ref, acc, dmat, pmat, slog, own_ref, par_ref, dst_ref, src_ref, cnt_ref,
                sem, far_sem, in_sem, q_ref, far_ref, bd_ref, m_ref, head_ref):
    nchunk = TILES // CHUNK

    def mask_copy(c):
        rows = pl.ds(c * CHUNK, CHUNK)
        return pltpu.make_async_copy(mask_hbm.at[rows], masks.at[rows], sem.at[c])

    def far_copy(c):
        rows = pl.ds(c * PART, PART)
        return pltpu.make_async_copy(far_hbm.at[rows], far_ref.at[rows], far_sem.at[c])

    inputs = [
        pltpu.make_async_copy(src, dst, in_sem.at[i])
        for i, (src, dst) in enumerate((
            (par_hbm, par_ref), (cnt_hbm, cnt_ref), (dst_hbm, dst_ref), (src_hbm, src_ref),
            (q_hbm, q_ref), (acc_hbm, acc), (own_hbm, own_ref)))
    ]
    inputs[0].start()
    for c in range(PEERS // PART):
        far_copy(c).start()
    for copy in inputs[1:]:
        copy.start()

    def start(c, _):
        mask_copy(c).start()
        return 0

    lax.fori_loop(0, nchunk, start, 0)
    inputs[0].wait()

    a_s = par_ref[0:8]
    a_d = par_ref[8:16]
    sig_col = par_ref[16:24]
    a24 = stacked3(a_s)
    pair = 2

    def far_scores(i, carry):
        low, high = carry
        p = i * pair
        raw = score_rows(a24, far_ref[pl.ds(p, pair)].reshape(pair * BLK, F))
        for k in range(pair):
            mine = raw[:, k * BLK:(k + 1) * BLK]
            part = mine - sig_col
            s_ref[p + k] = mine
            bf_ref[p + k] = jnp.exp(part)
            df_ref[p + k] = jnp.exp(0.2 * part)
            low = jnp.minimum(low, part)
            high = jnp.maximum(high, part)
        return low, high

    zero = jnp.zeros((HEADS, BLK), F32)

    def far_part(c, carry):
        far_copy(c).wait()
        for i in range(PART // pair):
            carry = far_scores(c * (PART // pair) + i, carry)
        return carry

    low, high = lax.fori_loop(0, PEERS // PART, far_part, (zero, zero))
    low = jnp.minimum(low, par_ref[32:40])
    bounded = jnp.logical_and(jnp.min(low) >= -LOW, jnp.max(high) <= HIGH)
    for copy in inputs[1:]:
        copy.wait()
    count = cnt_ref[0, 0]

    lane1 = iota((BLK, F), 1)
    head_ref[...] = (iota((ROWS, F), 1) // HD).astype(F32).astype(BF)
    cut = (BLK // ROWS, ROWS, F)

    def values(v):
        v = v.reshape(cut)
        head_id = head_ref[...]
        sides = []
        for half in range(2):
            parts = []
            for k in range(HEADS // 2):
                h = half * (HEADS // 2) + k
                mine = jnp.broadcast_to((head_id == h)[None], cut)
                ones = (head_id == (h + HEADS // 2) % HEADS).astype(F32).astype(BF)
                parts.append(jnp.where(mine, v, jnp.broadcast_to(ones[None], cut)).reshape(BLK, F))
            sides.append(jnp.concatenate(parts, axis=0))
        return sides

    def tile_sums(v, weight_of):
        sides = values(v)
        sums = []
        for half in range(2):
            w = jnp.concatenate([weight_of(half * (HEADS // 2) + k) for k in range(HEADS // 2)], axis=1)
            sums.append(jnp.dot(w, sides[half], preferred_element_type=F32))
        return sums

    def add_sums(dst, sums):
        for half in range(2):
            acc[dst, :, half * F:(half + 1) * F] += sums[half]

    @pl.when(bounded)
    def _():
        def chunk(c, _):
            mask_copy(c).wait()
            live = jnp.clip((count - c * CHUNK + GROUP - 1) // GROUP, 0, CHUNK // GROUP)

            def group(g, _):
                todo = []
                for k in range(GROUP):
                    t = c * CHUNK + g * GROUP + k
                    src = src_ref[0, t]
                    used = (t < count).astype(F32)
                    m_ref[k] = (masks[t].astype(F32) * used).astype(BF)
                    for h in range(HEADS):
                        bd_ref[k, 0, h] = jnp.broadcast_to(bf_ref[src, h:h + 1, :], (ROWS, BLK)).astype(BF)
                        bd_ref[k, 1, h] = jnp.broadcast_to(df_ref[src, h:h + 1, :], (ROWS, BLK)).astype(BF)
                for k in range(GROUP):
                    t = c * CHUNK + g * GROUP + k
                    dst = dst_ref[0, t]
                    src = src_ref[0, t]
                    m = m_ref[k].reshape(cut)

                    def weight_of(h):
                        q = q_ref[dst, h].reshape(cut)
                        bj = jnp.broadcast_to(bd_ref[k, 0, h][None], cut)
                        dj = jnp.broadcast_to(bd_ref[k, 1, h][None], cut)
                        return (jnp.maximum(q * bj, dj) * m).reshape(BLK, BLK)

                    todo.append((dst, tile_sums(far_ref[src], weight_of)))
                for dst, sums in todo:
                    add_sums(dst, sums)
                return 0

            lax.fori_loop(0, live, group, 0)
            return 0

        lax.fori_loop(0, nchunk, chunk, 0)

    @pl.when(jnp.logical_not(bounded))
    def _():
        def finish(c, _):
            mask_copy(c).wait()
            return 0

        lax.fori_loop(0, nchunk, finish, 0)

        for h in range(HEADS):
            dh = jnp.broadcast_to(a_d[h:h + 1], (F, F))
            sh = jnp.broadcast_to(a_s[h:h + 1], (F, F))

            def rows(b, _):
                ob = own_ref[pl.ds(b * BLK, BLK)]
                d = nt_exact(ob, dh)
                dmat[b, h] = d
                pmat[b, h] = leaky(d + nt_exact(ob, sh))
                return 0

            lax.fori_loop(0, NB, rows, 0)

        def expand(b):
            px = pmat[b, 0]
            for h in range(1, HEADS):
                px = jnp.where(lane1 // HD == h, pmat[b, h], px)
            return px

        def keep(b, _):
            slog[pl.ds(b * BLK, BLK)] = expand(b)
            return 0

        lax.fori_loop(0, NB, keep, 0)

        def peak(t, _):
            dst = dst_ref[0, t]
            src = src_ref[0, t]
            edge = masks[t] > 0
            for h in range(HEADS):
                lg = leaky(dmat[dst, h] + s_ref[src, h:h + 1, :])
                top = jnp.max(jnp.where(edge, lg, -jnp.inf), axis=1, keepdims=True)
                pmat[dst, h] = jnp.maximum(pmat[dst, h], top)
            return 0

        lax.fori_loop(0, count, peak, 0)

        def settle(b, _):
            rows = pl.ds(b * BLK, BLK)
            slog[rows] = jnp.exp(slog[rows] - expand(b))
            return 0

        lax.fori_loop(0, NB, settle, 0)
        self_sums(acc, own_ref[...], slog[...])

        def tile(t, _):
            dst = dst_ref[0, t]
            src = src_ref[0, t]
            edge = masks[t] > 0

            def weight_of(h):
                lg = leaky(dmat[dst, h] + s_ref[src, h:h + 1, :])
                return jnp.exp(jnp.where(edge, lg - pmat[dst, h], -jnp.inf)).astype(BF)

            add_sums(dst, tile_sums(far_ref[src], weight_of))
            return 0

        lax.fori_loop(0, count, tile, 0)

    bias = par_ref[24:25]
    for b in range(NB):
        one = acc[b, :, 0:F]
        two = acc[b, :, F:2 * F]
        left = lane1 < F // 2
        top = jnp.where(left, one, two)
        low_part = pltpu.roll(jnp.where(left, two, one), F // 2, 1)
        mixed = top / low_part + bias
        small = mixed * (1.0 + mixed * (0.5 + mixed * (1.0 / 6.0 + mixed * (1.0 / 24.0))))
        neg = jnp.where(mixed > -0.0625, small, jnp.exp(jnp.minimum(mixed, 0.0)) - 1.0)
        out_ref[pl.ds(b * BLK, BLK)] = jnp.where(mixed > 0, mixed, neg).astype(BF)


def attend(far, own, q, sums, params, dst, src, masks, count):
    vm = pl.BlockSpec(memory_space=pltpu.VMEM)
    hbm = pl.BlockSpec(memory_space=pltpu.HBM)
    return pl.pallas_call(
        attend_kernel,
        out_shape=jax.ShapeDtypeStruct((NB * BLK, F), BF),
        in_specs=[hbm] * 9,
        out_specs=vm,
        scratch_shapes=[
            pltpu.VMEM((TILES, BLK, BLK), jnp.int32),
            pltpu.VMEM((PEERS, HEADS, BLK), F32),
            pltpu.VMEM((PEERS, HEADS, BLK), F32),
            pltpu.VMEM((PEERS, HEADS, BLK), F32),
            pltpu.VMEM((NB, BLK, 2 * F), F32),
            pltpu.VMEM((NB, HEADS, BLK, F), F32),
            pltpu.VMEM((NB, HEADS, BLK, F), F32),
            pltpu.VMEM((NB * BLK, F), F32),
            pltpu.VMEM((NB * BLK, F), BF),
            pltpu.VMEM((40, F), F32),
            pltpu.SMEM((1, TILES), jnp.int32),
            pltpu.SMEM((1, TILES), jnp.int32),
            pltpu.SMEM((1, 1), jnp.int32),
            pltpu.SemaphoreType.DMA((TILES // CHUNK,)),
            pltpu.SemaphoreType.DMA((PEERS // PART,)),
            pltpu.SemaphoreType.DMA((7,)),
        ],
        compiler_params=pltpu.CompilerParams(vmem_limit_bytes=VMEM_ALL),
        name="attend",
    )(dst, src, count.reshape(1, 1), far, own, q, sums, params, masks)


SIDE = 4
SPLIT = (("z", "y", "x"), ("z", "x", "y"), ("y", "x", "z"), ("x", "y", "z"))
WAYS = len(SPLIT)
SPAN = BLK // WAYS
AXES = ("y", "z", "x")
OTHERS = tuple((off, flip) for off in (1, 3, 2) for flip in (0, 1))
LINE = ((0, 1),) + OTHERS
STEPS = (1, 3, 2)
TURNS = (0, 1, 3, 2)


def peer_list():
    peers = [("x", 0, 1)]
    for axis in AXES:
        for off, flip in OTHERS:
            peers.append((axis, off, flip))
    return peers


PEER_LIST = peer_list()


def peer_slot(axis, off, flip):
    if off == 0:
        return 0
    return PEER_LIST.index((axis, off, flip))


def place(pos, core):
    return ((pos["y"] * SIDE + pos["z"]) * SIDE + pos["x"]) * 2 + core


def exchange_kernel(x_hbm, w_hbm, req_hbm, atts_hbm, attd_hbm, bias_hbm,
                    far_ref, own_hbm, q_hbm, acc_hbm, par_hbm, *scratch):
    gathered = tuple(scratch[SIDE * c:SIDE * c + SIDE] for c in range(WAYS))
    picked = scratch[SIDE * WAYS:SIDE * WAYS + WAYS]
    (x_ref, w_ref, req_ref, atts_ref, attd_ref, bias_ref, req_s, rq, rqs, own_ref, q_out, acc_out, par_ref,
     fetch_sem, give_sem,
     ask_s, ask_r, one_s, one_r, two_s, two_r, fwd_s, fwd_r, out_s, out_r, local_sem, smem_sem) = (
        scratch[SIDE * WAYS + WAYS:])
    me = lax.axis_index("node")
    core = lax.rem(me, 2)
    pos = {
        "x": lax.rem(lax.div(me, 2), SIDE),
        "z": lax.rem(lax.div(me, 2 * SIDE), SIDE),
        "y": lax.div(me, 2 * SIDE * SIDE),
    }

    def shifted(axis, off):
        return lax.rem(pos[axis] + off, SIDE)

    def device(axis, off, flip):
        where = dict(pos)
        where[axis] = shifted(axis, off)
        return place(where, lax.rem(core + flip, 2))

    def send(src, dst, ssem, rsem, axis, off, flip):
        return pltpu.make_async_remote_copy(
            src_ref=src, dst_ref=dst, send_sem=ssem, recv_sem=rsem,
            device_id=(device(axis, off, flip),), device_id_type=pl.DeviceIdType.MESH,
        )

    fetches = [
        pltpu.make_async_copy(src, dst, fetch_sem.at[i])
        for i, (src, dst) in enumerate((
            (x_hbm, x_ref), (w_hbm, w_ref), (req_hbm, req_ref), (req_hbm, req_s),
            (atts_hbm, atts_ref), (attd_hbm, attd_ref), (bias_hbm, bias_ref)))
    ]
    for f in fetches:
        f.start()
    barrier = pltpu.get_barrier_semaphore()
    for axis, off, flip in PEER_LIST:
        pl.semaphore_signal(barrier, inc=1, device_id=(device(axis, off, flip),), device_id_type=pl.DeviceIdType.MESH)
    for f in fetches:
        f.wait()

    proj = jnp.dot(x_ref[...], w_ref[...], preferred_element_type=F32).astype(BF)
    own_ref[...] = proj
    blocks = proj.reshape(NB, BLK, F)
    for c, (ga, gb, gf) in enumerate(SPLIT):
        gathered[c][0][pos[ga]] = blocks[:, c * SPAN:(c + 1) * SPAN]

    pl.semaphore_wait(barrier, len(PEER_LIST))

    def ask(i):
        axis, off, flip = PEER_LIST[i]
        return send(req_ref, rq.at[i], ask_s.at[i], ask_r.at[i], axis, off, flip)

    def first(c, i, back=False):
        ga = SPLIT[c][0]
        off = STEPS[i]
        mine = gathered[c][0].at[pos[ga]]
        dst = gathered[c][0].at[shifted(ga, SIDE - off)] if back else mine
        return send(mine, dst, one_s.at[c, i], one_r.at[c, i], ga, off, 0)

    def second(c, k, i):
        ga, gb = SPLIT[c][:2]
        at = shifted(ga, (SIDE - TURNS[k]) % SIDE)
        return send(gathered[c][0].at[at], gathered[c][i + 1].at[at], two_s.at[c, k, i], two_r.at[c, k, i],
                    gb, STEPS[i], 0)

    def onward(c, k, i):
        ga, gb = SPLIT[c][:2]
        at = shifted(ga, (SIDE - TURNS[k]) % SIDE)
        part = pl.ds(i * (NB // 2), NB // 2)
        return send(gathered[c][i + 1].at[at, part], gathered[c][3].at[at, part], fwd_s.at[c, k, i], fwd_r.at[c, k, i],
                    gb, STEPS[i], 0)

    def landing(c, b_at, f_at, from_core):
        ga, gb, gf = SPLIT[c]
        spot = {ga: pl.ds(0, SIDE), gb: b_at, gf: f_at}
        return far_ref.at[spot["y"], spot["z"], spot["x"], from_core, pl.ds(c * SPAN, SPAN)]

    def third(c, q, j, back=False):
        ga, gb, gf = SPLIT[c]
        off, flip = LINE[j]
        b_at = shifted(gb, (SIDE - TURNS[q]) % SIDE)
        if back:
            dst = landing(c, b_at, shifted(gf, (SIDE - off) % SIDE), lax.rem(core + flip, 2))
        else:
            dst = landing(c, b_at, pos[gf], core)
        return send(picked[c].at[q, j], dst, out_s.at[c, q, j], out_r.at[c, q, j], gf, off, flip)

    def stay(c, q):
        gb, gf = SPLIT[c][1:3]
        b_at = shifted(gb, (SIDE - TURNS[q]) % SIDE)
        return pltpu.make_async_copy(picked[c].at[q, len(LINE)], landing(c, b_at, pos[gf], core), local_sem.at[c, q])

    for i in range(3):
        for c in range(WAYS):
            first(c, i).start()
    for i in range(len(PEER_LIST)):
        ask(i).start()
    for i in range(2):
        for c in range(WAYS):
            second(c, 0, i).start()

    own_head = iota((HEADS, F), 1) // HD == iota((HEADS, F), 0)

    def spread(att):
        return jnp.where(own_head, jnp.concatenate([att] * HEADS, axis=1), 0.0)

    a_s = spread(atts_ref[...])
    a_d = spread(attd_ref[...])
    own = own_ref[...]
    own_s = score_rows(stacked3(a_s), own)
    sig_col = jnp.max(own_s, axis=1, keepdims=True)
    sig_x = jnp.sum(jnp.where(own_head, sig_col, 0.0), axis=0, keepdims=True)
    par_ref[0:8] = a_s
    par_ref[8:16] = a_d
    par_ref[16:24] = jnp.broadcast_to(sig_col, (HEADS, F))
    par_ref[24:32] = jnp.broadcast_to(bias_ref[...], (8, F))
    par_ref[32:40] = jnp.broadcast_to(jnp.min(own_s - sig_col, axis=1, keepdims=True), (HEADS, F))

    same_head = iota((F, F), 0) // HD == iota((F, F), 1) // HD
    sx = nt_exact(own, jnp.where(same_head, jnp.sum(a_s, axis=0, keepdims=True), 0.0))
    dx = nt_exact(own, jnp.where(same_head, jnp.sum(a_d, axis=0, keepdims=True), 0.0))
    qx = jnp.exp(0.8 * jnp.minimum(dx + sig_x, LOW)).astype(BF)
    for h in range(HEADS):
        pick_col = (iota((F, F), 0) == h * HD).astype(F32).astype(BF)
        q_out[:, h] = jnp.dot(qx, pick_col, preferred_element_type=F32).astype(BF).reshape(NB, BLK, F)
    xo = sx - sig_x
    self_sums(acc_out, own, jnp.maximum(qx.astype(F32) * jnp.exp(xo), jnp.exp(0.2 * xo)))
    gives = [
        pltpu.make_async_copy(src, dst, give_sem.at[i])
        for i, (src, dst) in enumerate(((own_ref, own_hbm), (q_out, q_hbm), (acc_out, acc_hbm), (par_ref, par_hbm)))
    ]
    for g in gives:
        g.start()

    for k in range(1, SIDE):
        for c in range(WAYS):
            first(c, k - 1, True).wait_recv()
            for i in range(2):
                second(c, k, i).start()
    for i in range(len(PEER_LIST)):
        ask(i).wait_recv()
    fetch = pltpu.make_async_copy(rq, rqs, smem_sem.at[0])
    fetch.start()
    fetch.wait()

    def pick(c, q):
        ga, gb, gf = SPLIT[c]
        b_at = shifted(gb, (SIDE - TURNS[q]) % SIDE)
        for j in range(len(LINE) + 1):
            for a_at in range(SIDE):
                col = place({ga: a_at, gb: b_at, gf: pos[gf]}, core)
                if j < len(LINE):
                    off, flip = LINE[j]
                    block = rqs[peer_slot(gf, (SIDE - off) % SIDE, flip), 0, col]
                else:
                    block = req_s[0, col]
                picked[c][q, j, a_at] = gathered[c][q][a_at, block]

    for q in range(SIDE):
        for c in range(WAYS):
            for k in range(SIDE):
                if q in (1, 2):
                    second(c, k, q - 1).wait_recv()
                    onward(c, k, q - 1).start()
                if q == 3:
                    onward(c, k, 0).wait_recv()
                    onward(c, k, 1).wait_recv()
            pick(c, q)
            for j in range(len(LINE)):
                third(c, q, j).start()
            stay(c, q).start()

    for q in range(SIDE):
        for c in range(WAYS):
            for j in range(len(LINE)):
                third(c, q, j, True).wait_recv()
            stay(c, q).wait()
    for g in gives:
        g.wait()
    for i in range(len(PEER_LIST)):
        ask(i).wait_send()
    for c in range(WAYS):
        for i in range(3):
            first(c, i).wait_send()
        for q in range(SIDE):
            for i in range(2):
                second(c, q, i).wait_send()
                onward(c, q, i).wait_send()
            for j in range(len(LINE)):
                third(c, q, j).wait_send()


def exchange(x, weight, requests, att_src, att_dst, out_bias):
    hbm = pl.BlockSpec(memory_space=pltpu.HBM)
    dma = pltpu.SemaphoreType.DMA
    peers = len(PEER_LIST)
    lines = len(LINE)
    return pl.pallas_call(
        exchange_kernel,
        out_shape=(
            jax.ShapeDtypeStruct((SIDE, SIDE, SIDE, 2, BLK, F), BF),
            jax.ShapeDtypeStruct((NB * BLK, F), BF),
            jax.ShapeDtypeStruct((NB, HEADS, BLK, F), BF),
            jax.ShapeDtypeStruct((NB, BLK, 2 * F), F32),
            jax.ShapeDtypeStruct((40, F), F32),
        ),
        in_specs=[hbm] * 6,
        out_specs=(hbm,) * 5,
        scratch_shapes=(
            [pltpu.VMEM((SIDE, NB, SPAN, F), BF) for _ in range(WAYS * SIDE)]
            + [pltpu.VMEM((SIDE, lines + 1, SIDE, SPAN, F), BF) for _ in range(WAYS)]
            + [
                pltpu.VMEM((NB * BLK, F), BF),
                pltpu.VMEM((F, F), BF),
                pltpu.VMEM((1, PEERS), jnp.int32),
                pltpu.VMEM((HEADS, HD), F32),
                pltpu.VMEM((HEADS, HD), F32),
                pltpu.VMEM((1, F), F32),
                pltpu.SMEM((1, PEERS), jnp.int32),
                pltpu.VMEM((peers, 1, PEERS), jnp.int32),
                pltpu.SMEM((peers, 1, PEERS), jnp.int32),
                pltpu.VMEM((NB * BLK, F), BF),
                pltpu.VMEM((NB, HEADS, BLK, F), BF),
                pltpu.VMEM((NB, BLK, 2 * F), F32),
                pltpu.VMEM((40, F), F32),
                dma((7,)), dma((4,)),
                dma((peers,)), dma((peers,)),
                dma((WAYS, 3)), dma((WAYS, 3)),
                dma((WAYS, SIDE, 2)), dma((WAYS, SIDE, 2)),
                dma((WAYS, SIDE, 2)), dma((WAYS, SIDE, 2)),
                dma((WAYS, SIDE, lines)), dma((WAYS, SIDE, lines)),
                dma((WAYS, SIDE)), dma((1,)),
            ]
        ),
        compiler_params=pltpu.CompilerParams(
            collective_id=0, has_side_effects=True, vmem_limit_bytes=VMEM_ALL
        ),
        name="exchange",
    )(x, weight, requests, att_src, att_dst, out_bias.reshape(1, F))


def local(node_feats, weight, att_src, att_dst, out_bias, requests, tile_dst, tile_src, tile_masks, tile_count):
    far, own, q, sums, params = exchange(node_feats, weight, requests, att_src, att_dst, out_bias)
    far = far.reshape(PEERS, BLK, F)
    return attend(far, own, q, sums, params, tile_dst, tile_src, tile_masks[0], tile_count)


def solution(mesh):
    placed = (
        P("node", None), P(), P(), P(), P(), P("node", None), P("node", None), P("node", None),
        P("node", None, None, None), P("node"),
    )
    return jax.shard_map(local, mesh=mesh, in_specs=placed, out_specs=P("node", None), check_vma=False)
```

time: 143 us -> 139 us (0.972)
  the two profiles are of different devices: /device:TPU:4 before, /device:TPU:5 now
where the time goes in v2:
time: 139 us; the launch traced here: 138 us
  Pallas kernels  137 us (99%)
    pallas_call x1, Pallas kernels, attend(): pl.pallas_call(attend_kernel, out_shape=jax.ShapeDtypeStruct((NB * BLK, F...  89.2 us
    pallas_call x1, Pallas kernels, exchange(): pl.pallas_call(exchange_kernel, out_shape=(jax.ShapeDtypeStruct((SIDE, SI...  48.3 us

profile of v2, /device:TPU:5, one launch (start us, length us, event | category | flops | bytes accessed | tf_op | source)
XLA Modules:
  0.0 138.1 jit_solution(7641887872513135798)
XLA Ops:
  0.7 48.3 %exchange.1 = (bf16[4,4,4,2,128,128]{5,4,3,2,1,0:T(8,128)(2,1)}, bf16[1024,128]{1,0:T(8,128)(2,1)}, bf16[8,8,128,128]{3,2,1,0:T(8,128)(2,1)}, f32[8,128,256]{2,1,0:T(8,128)}, f32[40,128]{1,0:T(8,128)}) custom-call(bf16[1024,128]{1,0:T(8,128)(2,1)} %x_hbm.1, bf16[128,128]{1,0:T(8,128)(2,1)} %w_hbm.1, s32[1,128]{1,0:T(1,128)} %req_hbm.1, f32[8,16]{1,0:T(8,128)} %atts_hbm.1, ...), custom_call_target="tpu_custom_call" | custom-call | tf_op jit(solution)/shard_map/exchange/pallas_call | solution.py:563
  48.9 89.2 %attend.1 = bf16[1024,128]{1,0:T(8,128)(2,1)} custom-call(s32[1,128]{1,0:T(1,128)} %dst_hbm.1, s32[1,128]{1,0:T(1,128)} %src_hbm.1, s32[1,1]{1,0:T(1,128)} %bitcast.4.cnt_hbm, bf16[128,128,128]{2,1,0:T(8,128)(2,1)} %bitcast.6, bf16[1024,128]{1,0:T(8,128)(2,1)} %get-tuple-element.11.own_hbm, bf16[8,8,128,128]{3,2,1,0:T(8,128)(2,1)} %get-tuple-element.12.q_hbm, ...), custom_call_target="tpu_custom_call" | custom-call | tf_op jit(solution)/shard_map/attend/pallas_call | solution.py:302

commit v3 on v2

--- a/solution.py
+++ b/solution.py
@@ -14,8 +14,8 @@
 NB = 8
 TILES = 128
 PEERS = 128
-CHUNK = 8
-GROUP = 4
+CHUNK = 16
+GROUP = 16
 PART = 16
 VMEM_ALL = 67043328
 ROWS = 16
@@ -328,9 +328,10 @@
 
 
 SIDE = 4
-SPLIT = (("z", "y", "x"), ("z", "x", "y"), ("y", "x", "z"), ("x", "y", "z"))
+SPLIT = (("z", "y", "x"), ("x", "z", "y"), ("y", "x", "z"))
+ROW_AT = (0, 48, 96)
+SPANS = (48, 48, 32)
 WAYS = len(SPLIT)
-SPAN = BLK // WAYS
 AXES = ("y", "z", "x")
 OTHERS = tuple((off, flip) for off in (1, 3, 2) for flip in (0, 1))
 LINE = ((0, 1),) + OTHERS
@@ -407,7 +408,7 @@
     own_ref[...] = proj
     blocks = proj.reshape(NB, BLK, F)
     for c, (ga, gb, gf) in enumerate(SPLIT):
-        gathered[c][0][pos[ga]] = blocks[:, c * SPAN:(c + 1) * SPAN]
+        gathered[c][0][pos[ga]] = blocks[:, ROW_AT[c]:ROW_AT[c] + SPANS[c]]
 
     pl.semaphore_wait(barrier, len(PEER_LIST))
 
@@ -438,7 +439,7 @@
     def landing(c, b_at, f_at, from_core):
         ga, gb, gf = SPLIT[c]
         spot = {ga: pl.ds(0, SIDE), gb: b_at, gf: f_at}
-        return far_ref.at[spot["y"], spot["z"], spot["x"], from_core, pl.ds(c * SPAN, SPAN)]
+        return far_ref.at[spot["y"], spot["z"], spot["x"], from_core, pl.ds(ROW_AT[c], SPANS[c])]
 
     def third(c, q, j, back=False):
         ga, gb, gf = SPLIT[c]
@@ -535,11 +536,6 @@
                 third(c, q, j).start()
             stay(c, q).start()
 
-    for q in range(SIDE):
-        for c in range(WAYS):
-            for j in range(len(LINE)):
-                third(c, q, j, True).wait_recv()
-            stay(c, q).wait()
     for g in gives:
         g.wait()
     for i in range(len(PEER_LIST)):
@@ -551,8 +547,15 @@
             for i in range(2):
                 second(c, q, i).wait_send()
                 onward(c, q, i).wait_send()
+    for q in range(SIDE):
+        for c in range(WAYS):
             for j in range(len(LINE)):
                 third(c, q, j).wait_send()
+            stay(c, q).wait()
+    for q in range(SIDE):
+        for c in range(WAYS):
+            for j in range(len(LINE)):
+                third(c, q, j, True).wait_recv()
 
 
 def exchange(x, weight, requests, att_src, att_dst, out_bias):
@@ -572,8 +575,8 @@
         in_specs=[hbm] * 6,
         out_specs=(hbm,) * 5,
         scratch_shapes=(
-            [pltpu.VMEM((SIDE, NB, SPAN, F), BF) for _ in range(WAYS * SIDE)]
-            + [pltpu.VMEM((SIDE, lines + 1, SIDE, SPAN, F), BF) for _ in range(WAYS)]
+            [pltpu.VMEM((SIDE, NB, span, F), BF) for span in SPANS for _ in range(SIDE)]
+            + [pltpu.VMEM((SIDE, lines + 1, SIDE, span, F), BF) for span in SPANS]
             + [
                 pltpu.VMEM((NB * BLK, F), BF),
                 pltpu.VMEM((F, F), BF),

time: 139 us -> 135 us (0.971)
  the two profiles are of different devices: /device:TPU:5 before, /device:TPU:7 now
where the time goes in v3:
time: 135 us; the launch traced here: 134 us
  Pallas kernels  133 us (99%)
    pallas_call x1, Pallas kernels, attend(): pl.pallas_call(attend_kernel, out_shape=jax.ShapeDtypeStruct((NB * BLK, F...  89.2 us
    pallas_call x1, Pallas kernels, exchange(): pl.pallas_call(exchange_kernel, out_shape=(jax.ShapeDtypeStruct((SIDE, SI...  43.9 us

profile of v3, /device:TPU:7, one launch (start us, length us, event | category | flops | bytes accessed | tf_op | source)
XLA Modules:
  0.0 133.7 jit_solution(15606507317126626417)
XLA Ops:
  0.7 43.9 %exchange.1 = (bf16[4,4,4,2,128,128]{5,4,3,2,1,0:T(8,128)(2,1)}, bf16[1024,128]{1,0:T(8,128)(2,1)}, bf16[8,8,128,128]{3,2,1,0:T(8,128)(2,1)}, f32[8,128,256]{2,1,0:T(8,128)}, f32[40,128]{1,0:T(8,128)}) custom-call(bf16[1024,128]{1,0:T(8,128)(2,1)} %x_hbm.1, bf16[128,128]{1,0:T(8,128)(2,1)} %w_hbm.1, s32[1,128]{1,0:T(1,128)} %req_hbm.1, f32[8,16]{1,0:T(8,128)} %atts_hbm.1, ...), custom_call_target="tpu_custom_call" | custom-call | tf_op jit(solution)/shard_map/exchange/pallas_call | solution.py:566
  44.6 89.2 %attend.1 = bf16[1024,128]{1,0:T(8,128)(2,1)} custom-call(s32[1,128]{1,0:T(1,128)} %dst_hbm.1, s32[1,128]{1,0:T(1,128)} %src_hbm.1, s32[1,1]{1,0:T(1,128)} %bitcast.4.cnt_hbm, bf16[128,128,128]{2,1,0:T(8,128)(2,1)} %bitcast.6, bf16[1024,128]{1,0:T(8,128)(2,1)} %get-tuple-element.11.own_hbm, bf16[8,8,128,128]{3,2,1,0:T(8,128)(2,1)} %get-tuple-element.12.q_hbm, ...), custom_call_target="tpu_custom_call" | custom-call | tf_op jit(solution)/shard_map/attend/pallas_call | solution.py:302

commit v4 on v3

v4 whole, which is shorter than its diff:
```python
import functools

import jax
import jax.numpy as jnp
from jax import lax
from jax.experimental import pallas as pl
from jax.experimental.pallas import tpu as pltpu
from jax.sharding import PartitionSpec as P

HEADS = 8
HD = 16
F = 128
BLK = 128
NB = 8
TILES = 128
PEERS = 128
GROUP = 16
PART = 32
J = BLK // 2
GROUPS = TILES // GROUP
VMEM_ALL = 67043328
ROWS = 16
BF = jnp.bfloat16
F32 = jnp.float32
LOW = 40.0
HIGH = 30.0
NT = (((1,), (1,)), ((), ()))


def leaky(v):
    return jnp.maximum(v, 0.2 * v)


def nt_dot(a, b):
    return lax.dot_general(a, b, NT, preferred_element_type=F32)


def split3(a):
    hi = a.astype(BF)
    r1 = a - hi.astype(F32)
    mid = r1.astype(BF)
    lo = (r1 - mid.astype(F32)).astype(BF)
    return hi, mid, lo


def nt_exact(a, b):
    hi, mid, lo = split3(b)
    return (nt_dot(a, lo) + nt_dot(a, mid)) + nt_dot(a, hi)


def stacked3(a):
    return jnp.concatenate([part.astype(F32) for part in split3(a)], axis=0).astype(BF)


def score_rows(a24, blocks):
    r = nt_dot(a24, blocks)
    return (r[16:24] + r[8:16]) + r[0:8]


def self_sums(acc, own, w):
    first_half = lax.broadcasted_iota(jnp.int32, (NB * BLK, F), 1) < F // 2
    turned = pltpu.roll(w, F // 2, 1)
    wv = w * own.astype(F32)
    acc[:, :, 0:F] = jnp.where(first_half, wv, turned).reshape(NB, BLK, F)
    acc[:, :, F:2 * F] = jnp.where(first_half, turned, wv).reshape(NB, BLK, F)


def iota(shape, dim):
    return lax.broadcasted_iota(jnp.int32, shape, dim)


def halves_joined(x):
    left = iota((HEADS, BLK), 1) < J
    turned = pltpu.roll(x, J, 1)
    zero = jnp.where(left, x, pltpu.roll(turned, HEADS - 1, 0))
    one = jnp.where(left, turned, pltpu.roll(x, HEADS - 1, 0))
    return zero, one


def half_scores(far, a24, sig_col, b_ref, d_ref, first, count, carry):
    low, high = carry
    for i in range(count // 2):
        p = first + 2 * i
        x = score_rows(a24, far[pl.ds(p, 2)].reshape(BLK, F)) - sig_col
        low = jnp.minimum(low, x)
        high = jnp.maximum(high, x)
        for ref, e in ((b_ref, jnp.exp(x)), (d_ref, jnp.exp(0.2 * x))):
            ref[p], ref[p + 1] = halves_joined(e)
    return low, high


def half_tile(k, dst, q_ref, v, m, bd_ref, head_id, ones_ref):
    cut = (BLK // ROWS, ROWS, F)
    small = (J // ROWS, ROWS, F)
    v = v.reshape(small)
    m = m.reshape(cut)
    sums = []
    for side in range(2):
        weights = []
        for pair in range(2):
            at = side * 2 + pair
            q = q_ref[dst, at].reshape(cut)
            bj = jnp.broadcast_to(bd_ref[k, 0, at][None], cut)
            dj = jnp.broadcast_to(bd_ref[k, 1, at][None], cut)
            weights.append((jnp.maximum(q * bj, dj) * m).reshape(BLK, BLK))
        values = []
        for i in range(HEADS // 2):
            h = side * (HEADS // 2) + i
            mine = jnp.broadcast_to((head_id == h)[None], small)
            values.append(jnp.where(mine, v, jnp.broadcast_to(ones_ref[h][None], small)).reshape(J, F))
        sums.append(jnp.dot(jnp.concatenate(weights, axis=1), jnp.concatenate(values, axis=0),
                            preferred_element_type=F32))
    return sums


def lane_marks(head_ref, ones_ref):
    lane_head = iota((ROWS, F), 1) // HD
    head_ref[...] = lane_head.astype(F32).astype(BF)
    for h in range(HEADS):
        ones_ref[h] = (lane_head == (h + HEADS // 2) % HEADS).astype(F32).astype(BF)


def factor_rows(k, src, b_ref, d_ref, bd_ref):
    for at in range(HEADS // 2):
        bd_ref[k, 0, at] = jnp.broadcast_to(b_ref[src, 2 * at:2 * at + 1, :], (ROWS, BLK)).astype(BF)
        bd_ref[k, 1, at] = jnp.broadcast_to(d_ref[src, 2 * at:2 * at + 1, :], (ROWS, BLK)).astype(BF)


def attend_kernel(dst_hbm, src_hbm, cnt_hbm, fara_hbm, farb_hbm, own_hbm, q_hbm, acc_hbm, par_hbm, mb_hbm, part_hbm,
                  mask_hbm, out_ref, *scratch):
    pl.run_scoped(
        functools.partial(attend_body, dst_hbm, src_hbm, cnt_hbm, fara_hbm, farb_hbm, own_hbm, q_hbm, acc_hbm, par_hbm,
                          mb_hbm, part_hbm, mask_hbm, out_ref, *scratch),
        pltpu.VMEM((NB, HEADS // 2, BLK, F), BF),
        pltpu.VMEM((PEERS, J, F), BF),
        pltpu.VMEM((GROUP, 2, HEADS // 2, ROWS, F), BF),
        pltpu.VMEM((TILES, BLK, BLK), BF),
        pltpu.VMEM((TILES, BLK, 2 * F), BF),
        pltpu.VMEM((ROWS, F), BF),
        pltpu.VMEM((HEADS, ROWS, F), BF),
    )


def attend_body(dst_hbm, src_hbm, cnt_hbm, fara_hbm, farb_hbm, own_hbm, q_hbm, acc_hbm, par_hbm, mb_hbm, part_hbm,
                mask_hbm, out_ref, masks, fara_ref, s_ref, b_ref, d_ref, acc, dmat, pmat, slog, own_ref, par_ref,
                dst_ref, src_ref, cnt_ref, far_sem, in_sem, mb_sem, part_sem, late_sem,
                q_ref, far_ref, bd_ref, m_ref, part_ref, head_ref, ones_ref):
    def far_copy(c):
        rows = pl.ds(c * PART, PART)
        return pltpu.make_async_copy(farb_hbm.at[rows], far_ref.at[rows], far_sem.at[c])

    def group_copies(g):
        rows = pl.ds(g * GROUP, GROUP)
        return (pltpu.make_async_copy(mb_hbm.at[rows], m_ref.at[rows], mb_sem.at[g]),
                pltpu.make_async_copy(part_hbm.at[rows], part_ref.at[rows], part_sem.at[g]))

    inputs = [
        pltpu.make_async_copy(src, dst, in_sem.at[i])
        for i, (src, dst) in enumerate((
            (par_hbm, par_ref), (cnt_hbm, cnt_ref), (dst_hbm, dst_ref), (src_hbm, src_ref),
            (q_hbm, q_ref), (acc_hbm, acc), (own_hbm, own_ref)))
    ]
    inputs[0].start()
    for c in range(PEERS // PART):
        far_copy(c).start()
    for copy in inputs[1:]:
        copy.start()
    for g in range(GROUPS):
        for copy in group_copies(g):
            copy.start()
    inputs[0].wait()

    a_s = par_ref[0:8]
    a_d = par_ref[8:16]
    sig_col = par_ref[16:24]
    a24 = stacked3(a_s)
    lane_marks(head_ref, ones_ref)

    def far_part(c, carry):
        far_copy(c).wait()
        return half_scores(far_ref, a24, sig_col, b_ref, d_ref, c * PART, PART, carry)

    low, high = lax.fori_loop(0, PEERS // PART, far_part, (par_ref[32:40], par_ref[40:48]))
    bounded = jnp.logical_and(jnp.min(low) >= -LOW, jnp.max(high) <= HIGH)
    for copy in inputs[1:]:
        copy.wait()
    count = cnt_ref[0, 0]
    lane1 = iota((BLK, F), 1)

    def group_wait(g, _):
        for copy in group_copies(g):
            copy.wait()
        return 0

    @pl.when(bounded)
    def _():
        live = jnp.clip((count + GROUP - 1) // GROUP, 0, GROUPS)

        def group(g, _):
            group_wait(g, 0)
            head_id = head_ref[...]
            for k in range(GROUP):
                factor_rows(k, src_ref[0, g * GROUP + k], b_ref, d_ref, bd_ref)
            for k in range(GROUP):
                t = g * GROUP + k
                dst = dst_ref[0, t]
                src = src_ref[0, t]
                sums = half_tile(k, dst, q_ref, far_ref[src], m_ref[t], bd_ref, head_id, ones_ref)
                for side in range(2):
                    cols = slice(side * F, (side + 1) * F)
                    acc[dst, :, cols] += sums[side] + part_ref[t, :, cols].astype(F32)
            return 0

        lax.fori_loop(0, live, group, 0)
        lax.fori_loop(live, GROUPS, group_wait, 0)

    @pl.when(jnp.logical_not(bounded))
    def _():
        lax.fori_loop(0, GROUPS, group_wait, 0)
        late = (pltpu.make_async_copy(mask_hbm, masks, late_sem.at[0]),
                pltpu.make_async_copy(fara_hbm, fara_ref, late_sem.at[1]))
        for copy in late:
            copy.start()
        for copy in late:
            copy.wait()
        sides = (fara_ref, far_ref)

        def raw_scores(i, _):
            for half in range(2):
                x = score_rows(a24, sides[half][pl.ds(2 * i, 2)].reshape(BLK, F))
                s_ref[half, 2 * i] = x
                s_ref[half, 2 * i + 1] = pltpu.roll(x, J, 1)
            return 0

        lax.fori_loop(0, PEERS // 2, raw_scores, 0)

        for h in range(HEADS):
            dh = jnp.broadcast_to(a_d[h:h + 1], (F, F))
            sh = jnp.broadcast_to(a_s[h:h + 1], (F, F))

            def rows(b, _):
                ob = own_ref[pl.ds(b * BLK, BLK)]
                d = nt_exact(ob, dh)
                dmat[b, h] = d
                pmat[b, h] = leaky(d + nt_exact(ob, sh))
                return 0

            lax.fori_loop(0, NB, rows, 0)

        def expand(b):
            px = pmat[b, 0]
            for h in range(1, HEADS):
                px = jnp.where(lane1 // HD == h, pmat[b, h], px)
            return px

        def keep(b, _):
            slog[pl.ds(b * BLK, BLK)] = expand(b)
            return 0

        lax.fori_loop(0, NB, keep, 0)

        def edges(t, half):
            m = masks[t].astype(F32)
            if half:
                m = pltpu.roll(m, J, 1)
            return jnp.logical_and(m > 0.5, lane1 < J)

        def peak(t, _):
            dst = dst_ref[0, t]
            src = src_ref[0, t]
            for half in range(2):
                edge = edges(t, half)
                for h in range(HEADS):
                    lg = leaky(dmat[dst, h] + s_ref[half, src, h:h + 1, :])
                    top = jnp.max(jnp.where(edge, lg, -jnp.inf), axis=1, keepdims=True)
                    pmat[dst, h] = jnp.maximum(pmat[dst, h], top)
            return 0

        lax.fori_loop(0, count, peak, 0)

        def settle(b, _):
            rows = pl.ds(b * BLK, BLK)
            slog[rows] = jnp.exp(slog[rows] - expand(b))
            return 0

        lax.fori_loop(0, NB, settle, 0)
        self_sums(acc, own_ref[...], slog[...])
        lane2 = iota((J, F), 1)

        def tile(t, _):
            dst = dst_ref[0, t]
            src = src_ref[0, t]
            for half in range(2):
                edge = edges(t, half)
                v = sides[half][src].astype(F32)
                full = jnp.concatenate([v, jnp.zeros((J, F), F32)], axis=0)
                for h in range(HEADS):
                    lg = leaky(dmat[dst, h] + s_ref[half, src, h:h + 1, :])
                    w = jnp.exp(jnp.where(edge, lg - pmat[dst, h], -jnp.inf)).astype(BF)
                    ones = jnp.where(lane1 // HD == (h + HEADS // 2) % HEADS, 1.0, 0.0)
                    r = jnp.where(lane1 // HD == h, full, ones).astype(BF)
                    at = (h // (HEADS // 2)) * F
                    acc[dst, :, at:at + F] += jnp.dot(w, r, preferred_element_type=F32)
            return 0

        lax.fori_loop(0, count, tile, 0)

    bias = par_ref[24:25]
    for b in range(NB):
        one = acc[b, :, 0:F]
        two = acc[b, :, F:2 * F]
        left = lane1 < F // 2
        top = jnp.where(left, one, two)
        low_part = pltpu.roll(jnp.where(left, two, one), F // 2, 1)
        mixed = top / low_part + bias
        small = mixed * (1.0 + mixed * (0.5 + mixed * (1.0 / 6.0 + mixed * (1.0 / 24.0))))
        neg = jnp.where(mixed > -0.0625, small, jnp.exp(jnp.minimum(mixed, 0.0)) - 1.0)
        out_ref[pl.ds(b * BLK, BLK)] = jnp.where(mixed > 0, mixed, neg).astype(BF)


def attend(dst, src, count, fara, farb, own, q, sums, params, masks_b, parts, masks):
    vm = pl.BlockSpec(memory_space=pltpu.VMEM)
    hbm = pl.BlockSpec(memory_space=pltpu.HBM)
    dma = pltpu.SemaphoreType.DMA
    return pl.pallas_call(
        attend_kernel,
        out_shape=jax.ShapeDtypeStruct((NB * BLK, F), BF),
        in_specs=[hbm] * 12,
        out_specs=vm,
        scratch_shapes=[
            pltpu.VMEM((TILES, BLK, BLK), jnp.int32),
            pltpu.VMEM((PEERS, J, F), BF),
            pltpu.VMEM((2, PEERS, HEADS, BLK), F32),
            pltpu.VMEM((PEERS, HEADS, BLK), F32),
            pltpu.VMEM((PEERS, HEADS, BLK), F32),
            pltpu.VMEM((NB, BLK, 2 * F), F32),
            pltpu.VMEM((NB, HEADS, BLK, F), F32),
            pltpu.VMEM((NB, HEADS, BLK, F), F32),
            pltpu.VMEM((NB * BLK, F), F32),
            pltpu.VMEM((NB * BLK, F), BF),
            pltpu.VMEM((48, F), F32),
            pltpu.SMEM((1, TILES), jnp.int32),
            pltpu.SMEM((1, TILES), jnp.int32),
            pltpu.SMEM((1, 1), jnp.int32),
            dma((PEERS // PART,)), dma((7,)), dma((GROUPS,)), dma((GROUPS,)), dma((2,)),
        ],
        compiler_params=pltpu.CompilerParams(vmem_limit_bytes=VMEM_ALL),
        name="attend",
    )(dst, src, count, fara, farb, own, q, sums, params, masks_b, parts, masks)


SIDE = 4
SPLIT = (("z", "y", "x"), ("x", "z", "y"), ("y", "x", "z")) * 2
ROW_AT = (0, 24, 48, 0, 24, 48)
SPANS = (24, 24, 16) * 2
WAYS = len(SPLIT)
EARLY = (0, 1, 2)
LATER = (3, 4, 5)
AXES = ("y", "z", "x")
OTHERS = tuple((off, flip) for off in (1, 3, 2) for flip in (0, 1))
LINE = ((0, 1),) + OTHERS
STEPS = (1, 3, 2)
TURNS = (0, 1, 3, 2)


def peer_list():
    peers = [("x", 0, 1)]
    for axis in AXES:
        for off, flip in OTHERS:
            peers.append((axis, off, flip))
    return peers


PEER_LIST = peer_list()


def peer_slot(axis, off, flip):
    if off == 0:
        return 0
    return PEER_LIST.index((axis, off, flip))


def place(pos, core):
    return ((pos["y"] * SIDE + pos["z"]) * SIDE + pos["x"]) * 2 + core


def exchange_kernel(x_hbm, w_hbm, req_hbm, atts_hbm, attd_hbm, bias_hbm, dst_hbm, src_hbm, cnt_hbm, mask_hbm, *refs):
    pl.run_scoped(
        functools.partial(exchange_body, x_hbm, w_hbm, req_hbm, atts_hbm, attd_hbm, bias_hbm, dst_hbm, src_hbm, cnt_hbm,
                          mask_hbm, *refs),
        pltpu.VMEM((NB, HEADS // 2, BLK, F), BF),
        pltpu.VMEM((GROUP, J, F), BF),
        pltpu.VMEM((GROUP, 2, HEADS // 2, ROWS, F), BF),
        pltpu.VMEM((TILES, BLK, BLK), BF),
        pltpu.VMEM((TILES, BLK, BLK), BF),
        pltpu.VMEM((TILES, BLK, 2 * F), BF),
        pltpu.VMEM((ROWS, F), BF),
        pltpu.VMEM((HEADS, ROWS, F), BF),
    )


def exchange_body(x_hbm, w_hbm, req_hbm, atts_hbm, attd_hbm, bias_hbm, dst_hbm, src_hbm, cnt_hbm, mask_hbm,
                  fara_hbm, farb_ref, own_hbm, q_hbm, acc_hbm, par_hbm, mb_hbm, part_hbm, *scratch):
    q_out, v_ref, bd_ref, ma_ref, mb_ref, part_ref, head_ref, ones_ref = scratch[-8:]
    scratch = scratch[:-8]
    gathered = tuple(scratch[SIDE * c:SIDE * c + SIDE] for c in range(WAYS))
    picked = scratch[SIDE * WAYS:SIDE * WAYS + WAYS]
    (x_ref, w_ref, req_ref, atts_ref, attd_ref, bias_ref, req_s, rq, rqs, own_ref, acc_out, par_ref,
     fara_ref, masks, b_ref, d_ref, dst_ref, src_ref, cnt_ref,
     fetch_sem, give_sem, mask_sem, mb_sem, part_sem,
     ask_s, ask_r, one_s, one_r, two_s, two_r, fwd_s, fwd_r, out_s, out_r, local_sem, smem_sem) = (
        scratch[SIDE * WAYS + WAYS:])
    me = lax.axis_index("node")
    core = lax.rem(me, 2)
    pos = {
        "x": lax.rem(lax.div(me, 2), SIDE),
        "z": lax.rem(lax.div(me, 2 * SIDE), SIDE),
        "y": lax.div(me, 2 * SIDE * SIDE),
    }

    def shifted(axis, off):
        return lax.rem(pos[axis] + off, SIDE)

    known = {}

    def device(axis, off, flip):
        key = (axis if off else "", off, flip)
        if key not in known:
            where = dict(pos)
            where[axis] = shifted(axis, off)
            known[key] = place(where, lax.rem(core + flip, 2))
        return known[key]

    def send(src, dst, ssem, rsem, axis, off, flip):
        return pltpu.make_async_remote_copy(
            src_ref=src, dst_ref=dst, send_sem=ssem, recv_sem=rsem,
            device_id=(device(axis, off, flip),), device_id_type=pl.DeviceIdType.MESH,
        )

    fetches = [
        pltpu.make_async_copy(src, dst, fetch_sem.at[i])
        for i, (src, dst) in enumerate((
            (x_hbm, x_ref), (w_hbm, w_ref), (req_hbm, req_ref), (req_hbm, req_s),
            (atts_hbm, atts_ref), (attd_hbm, attd_ref), (bias_hbm, bias_ref),
            (dst_hbm, dst_ref), (src_hbm, src_ref), (cnt_hbm, cnt_ref)))
    ]
    for f in fetches:
        f.start()
    barrier = pltpu.get_barrier_semaphore()
    for axis, off, flip in PEER_LIST:
        pl.semaphore_signal(barrier, inc=1, device_id=(device(axis, off, flip),), device_id_type=pl.DeviceIdType.MESH)
    for f in fetches:
        f.wait()

    proj = jnp.dot(x_ref[...], w_ref[...], preferred_element_type=F32).astype(BF)
    own_ref[...] = proj
    for c, (ga, gb, gf) in enumerate(SPLIT):
        for b in range(NB):
            at = b * BLK + (c // 3) * J + ROW_AT[c]
            gathered[c][0][pos[ga], b] = own_ref[pl.ds(at, SPANS[c])]

    pl.semaphore_wait(barrier, len(PEER_LIST))

    def ask(i):
        axis, off, flip = PEER_LIST[i]
        return send(req_ref, rq.at[i], ask_s.at[0], ask_r.at[0], axis, off, flip)

    def first(c, i, back=False):
        ga = SPLIT[c][0]
        off = STEPS[i]
        mine = gathered[c][0].at[pos[ga]]
        dst = gathered[c][0].at[shifted(ga, SIDE - off)] if back else mine
        return send(mine, dst, one_s.at[c], one_r.at[c, i], ga, off, 0)

    def second(c, k, i):
        ga, gb = SPLIT[c][:2]
        at = shifted(ga, (SIDE - TURNS[k]) % SIDE)
        return send(gathered[c][0].at[at], gathered[c][i + 1].at[at], two_s.at[c, i], two_r.at[c, k, i],
                    gb, STEPS[i], 0)

    def onward(c, k, i):
        ga, gb = SPLIT[c][:2]
        at = shifted(ga, (SIDE - TURNS[k]) % SIDE)
        part = pl.ds(i * (NB // 2), NB // 2)
        return send(gathered[c][i + 1].at[at, part], gathered[c][3].at[at, part], fwd_s.at[c, i], fwd_r.at[c],
                    gb, STEPS[i], 0)

    def landing(c, b_at, f_at, from_core):
        ga, gb, gf = SPLIT[c]
        spot = {ga: pl.ds(0, SIDE), gb: b_at, gf: f_at}
        far = farb_ref if c in LATER else fara_ref
        return far.at[spot["y"], spot["z"], spot["x"], from_core, pl.ds(ROW_AT[c], SPANS[c])]

    def third(c, q, j):
        ga, gb, gf = SPLIT[c]
        off, flip = LINE[j]
        b_at = shifted(gb, (SIDE - TURNS[q]) % SIDE)
        return send(picked[c].at[q, j], landing(c, b_at, pos[gf], core), out_s.at[c, q], out_r.at[c, q], gf, off, flip)

    def stay(c, q):
        gb, gf = SPLIT[c][1:3]
        b_at = shifted(gb, (SIDE - TURNS[q]) % SIDE)
        return pltpu.make_async_copy(picked[c].at[q, len(LINE)], landing(c, b_at, pos[gf], core), local_sem.at[c, q])

    def bulk(ref, ssem, rsem):
        return send(ref, ref, ssem, rsem, "x", 0, 1)

    def all_asks():
        return bulk(rq, ask_s.at[0], ask_r.at[0])

    def all_onward(c):
        return bulk(gathered[c][3], fwd_s.at[c, 0], fwd_r.at[c])

    def all_third(c, q):
        return bulk(picked[c].at[q, pl.ds(0, len(LINE))], out_s.at[c, q], out_r.at[c, q])

    def mask_copy(g):
        rows = pl.ds(g * GROUP, GROUP)
        return pltpu.make_async_copy(mask_hbm.at[rows], masks.at[rows], mask_sem.at[g])

    def group_gives(g):
        rows = pl.ds(g * GROUP, GROUP)
        return (pltpu.make_async_copy(mb_ref.at[rows], mb_hbm.at[rows], mb_sem.at[g]),
                pltpu.make_async_copy(part_ref.at[rows], part_hbm.at[rows], part_sem.at[g]))

    for i in range(3):
        for c in EARLY:
            first(c, i).start()
    for i in range(len(PEER_LIST)):
        ask(i).start()
    for i in range(2):
        for c in EARLY:
            second(c, 0, i).start()
    for i in range(3):
        for c in LATER:
            first(c, i).start()
    for g in range(GROUPS):
        mask_copy(g).start()

    own_head = iota((HEADS, F), 1) // HD == iota((HEADS, F), 0)

    def spread(att):
        return jnp.where(own_head, jnp.concatenate([att] * HEADS, axis=1), 0.0)

    a_s = spread(atts_ref[...])
    a_d = spread(attd_ref[...])
    own = own_ref[...]
    a24 = stacked3(a_s)
    own_s = score_rows(a24, own)
    sig_col = jnp.max(own_s, axis=1, keepdims=True)
    sig_x = jnp.sum(jnp.where(own_head, sig_col, 0.0), axis=0, keepdims=True)
    par_ref[0:8] = a_s
    par_ref[8:16] = a_d
    par_ref[16:24] = jnp.broadcast_to(sig_col, (HEADS, F))
    par_ref[24:32] = jnp.broadcast_to(bias_ref[...], (8, F))
    own_low = jnp.broadcast_to(jnp.min(own_s - sig_col, axis=1, keepdims=True), (HEADS, F))

    same_head = iota((F, F), 0) // HD == iota((F, F), 1) // HD
    sx = nt_exact(own, jnp.where(same_head, jnp.sum(a_s, axis=0, keepdims=True), 0.0))
    dx = nt_exact(own, jnp.where(same_head, jnp.sum(a_d, axis=0, keepdims=True), 0.0))
    qx = jnp.exp(0.8 * jnp.minimum(dx + sig_x, LOW)).astype(BF)
    for h in range(HEADS // 2):
        wanted_row = (2 * h + iota((F, F), 1) // J) * HD
        pick_col = (iota((F, F), 0) == wanted_row).astype(F32).astype(BF)
        q_out[:, h] = jnp.dot(qx, pick_col, preferred_element_type=F32).astype(BF).reshape(NB, BLK, F)
    xo = sx - sig_x
    self_sums(acc_out, own, jnp.maximum(qx.astype(F32) * jnp.exp(xo), jnp.exp(0.2 * xo)))
    gives = [
        pltpu.make_async_copy(src, dst, give_sem.at[i])
        for i, (src, dst) in enumerate(((own_ref, own_hbm), (q_out, q_hbm), (acc_out, acc_hbm)))
    ]
    for g in gives:
        g.start()

    def spread_second(ways):
        for k in range(1, SIDE):
            for c in ways:
                first(c, k - 1, True).wait_recv()
                for i in range(2):
                    second(c, k, i).start()

    spread_second(EARLY)
    for i in range(2):
        for c in LATER:
            second(c, 0, i).start()
    all_asks().wait_recv()
    fetch = pltpu.make_async_copy(rq, rqs, smem_sem.at[0])
    fetch.start()
    fetch.wait()

    def pick(c, q):
        ga, gb, gf = SPLIT[c]
        b_at = shifted(gb, (SIDE - TURNS[q]) % SIDE)
        for j in range(len(LINE) + 1):
            for a_at in range(SIDE):
                col = place({ga: a_at, gb: b_at, gf: pos[gf]}, core)
                if j < len(LINE):
                    off, flip = LINE[j]
                    block = rqs[peer_slot(gf, (SIDE - off) % SIDE, flip), 0, col]
                else:
                    block = req_s[0, col]
                part = gathered[c][q][a_at, block]
                if c in EARLY and j == len(LINE):
                    spot = {ga: a_at, gb: b_at, gf: pos[gf]}
                    fara_ref[spot["y"], spot["z"], spot["x"], core, pl.ds(ROW_AT[c], SPANS[c])] = part
                else:
                    picked[c][q, j, a_at] = part

    count = cnt_ref[0, 0]
    left = iota((BLK, BLK), 1) < J
    lane_marks(head_ref, ones_ref)

    def prepare(g, _):
        mask_copy(g).wait()
        for k in range(GROUP):
            t = g * GROUP + k
            m = masks[t].astype(F32) * (t < count).astype(F32)
            turned = pltpu.roll(m, J, 1)
            ma_ref[t] = jnp.where(left, m, turned).astype(BF)
            mb_ref[t] = jnp.where(left, turned, m).astype(BF)
        group_gives(g)[0].start()
        return 0

    def pass_on(c, q):
        for k in range(SIDE):
            second(c, k, q - 1).wait_recv()
            onward(c, k, q - 1).start()

    def hand_out(c, q):
        pick(c, q)
        for j in range(len(LINE)):
            third(c, q, j).start()
        if c in LATER:
            stay(c, q).start()

    for c in EARLY:
        hand_out(c, 0)
    lax.fori_loop(0, GROUPS // 2, prepare, 0)
    spread_second(LATER)
    for q in (1, 2):
        for c in EARLY:
            pass_on(c, q)
            hand_out(c, q)
    lax.fori_loop(GROUPS // 2, GROUPS, prepare, 0)
    for c in EARLY:
        all_onward(c).wait_recv()
        hand_out(c, 3)
    for q in (1, 2):
        for c in LATER:
            pass_on(c, q)
    for q in (0, 1, 2):
        for c in LATER:
            hand_out(c, q)
    for c in LATER:
        all_onward(c).wait_recv()
        hand_out(c, 3)

    for q in range(SIDE):
        for c in EARLY:
            all_third(c, q).wait_recv()

    def far_part(c, carry):
        p = c * PART
        return half_scores(fara_flat, a24, sig_col, b_ref, d_ref, p, PART, carry)

    fara_flat = fara_ref.reshape(PEERS, J, F)
    low, high = lax.fori_loop(0, PEERS // PART, far_part, (own_low, jnp.zeros((HEADS, F), F32)))
    par_ref[32:40] = low
    par_ref[40:48] = high
    last = (pltpu.make_async_copy(par_ref, par_hbm, give_sem.at[3]),
            pltpu.make_async_copy(fara_ref, fara_hbm, give_sem.at[4]))
    for copy in last:
        copy.start()

    def group(g, _):
        head_id = head_ref[...]
        for k in range(GROUP):
            src = src_ref[0, g * GROUP + k]
            v_ref[k] = fara_flat[src]
            factor_rows(k, src, b_ref, d_ref, bd_ref)
        for k in range(GROUP):
            t = g * GROUP + k
            sums = half_tile(k, dst_ref[0, t], q_out, v_ref[k], ma_ref[t], bd_ref, head_id, ones_ref)
            for side in range(2):
                part_ref[t, :, side * F:(side + 1) * F] = sums[side].astype(BF)
        group_gives(g)[1].start()
        return 0

    lax.fori_loop(0, GROUPS, group, 0)

    for g in gives:
        g.wait()
    for copy in last:
        copy.wait()
    all_asks().wait_send()
    for c in range(WAYS):
        bulk(gathered[c][0].at[pl.ds(0, 3)], one_s.at[c], one_r.at[c, 0]).wait_send()
        for i in range(2):
            bulk(gathered[c][i + 1], two_s.at[c, i], two_r.at[c, 0, 0]).wait_send()
            bulk(gathered[c][3].at[:, pl.ds(0, NB // 2)], fwd_s.at[c, i], fwd_r.at[c]).wait_send()
    for g in range(GROUPS):
        for copy in group_gives(g):
            copy.wait()
    for q in range(SIDE):
        for c in range(WAYS):
            all_third(c, q).wait_send()
        for c in LATER:
            stay(c, q).wait()
    for q in range(SIDE):
        for c in LATER:
            all_third(c, q).wait_recv()


def exchange(x, weight, requests, att_src, att_dst, out_bias, dst, src, count, masks):
    hbm = pl.BlockSpec(memory_space=pltpu.HBM)
    dma = pltpu.SemaphoreType.DMA
    peers = len(PEER_LIST)
    lines = len(LINE)
    far = (SIDE, SIDE, SIDE, 2, J, F)
    return pl.pallas_call(
        exchange_kernel,
        out_shape=(
            jax.ShapeDtypeStruct(far, BF),
            jax.ShapeDtypeStruct(far, BF),
            jax.ShapeDtypeStruct((NB * BLK, F), BF),
            jax.ShapeDtypeStruct((NB, HEADS // 2, BLK, F), BF),
            jax.ShapeDtypeStruct((NB, BLK, 2 * F), F32),
            jax.ShapeDtypeStruct((48, F), F32),
            jax.ShapeDtypeStruct((TILES, BLK, BLK), BF),
            jax.ShapeDtypeStruct((TILES, BLK, 2 * F), BF),
        ),
        in_specs=[hbm] * 10,
        out_specs=(hbm,) * 8,
        scratch_shapes=(
            [pltpu.VMEM((SIDE, NB, span, F), BF) for span in SPANS for _ in range(SIDE)]
            + [pltpu.VMEM((SIDE, lines + 1, SIDE, span, F), BF) for span in SPANS]
            + [
                pltpu.VMEM((NB * BLK, F), BF),
                pltpu.VMEM((F, F), BF),
                pltpu.VMEM((1, PEERS), jnp.int32),
                pltpu.VMEM((HEADS, HD), F32),
                pltpu.VMEM((HEADS, HD), F32),
                pltpu.VMEM((1, F), F32),
                pltpu.SMEM((1, PEERS), jnp.int32),
                pltpu.VMEM((peers, 1, PEERS), jnp.int32),
                pltpu.SMEM((peers, 1, PEERS), jnp.int32),
                pltpu.VMEM((NB * BLK, F), BF),
                pltpu.VMEM((NB, BLK, 2 * F), F32),
                pltpu.VMEM((48, F), F32),
                pltpu.VMEM(far, BF),
                pltpu.VMEM((TILES, BLK, BLK), jnp.int32),
                pltpu.VMEM((PEERS, HEADS, BLK), F32),
                pltpu.VMEM((PEERS, HEADS, BLK), F32),
                pltpu.SMEM((1, TILES), jnp.int32),
                pltpu.SMEM((1, TILES), jnp.int32),
                pltpu.SMEM((1, 1), jnp.int32),
                dma((10,)), dma((5,)), dma((GROUPS,)), dma((GROUPS,)), dma((GROUPS,)),
                dma((1,)), dma((1,)),
                dma((WAYS,)), dma((WAYS, 3)),
                dma((WAYS, 2)), dma((WAYS, SIDE, 2)),
                dma((WAYS, 2)), dma((WAYS,)),
                dma((WAYS, SIDE)), dma((WAYS, SIDE)),
                dma((WAYS, SIDE)), dma((1,)),
            ]
        ),
        compiler_params=pltpu.CompilerParams(
            collective_id=0, has_side_effects=True, vmem_limit_bytes=VMEM_ALL
        ),
        name="exchange",
    )(x, weight, requests, att_src, att_dst, out_bias.reshape(1, F), dst, src, count, masks)


def local(node_feats, weight, att_src, att_dst, out_bias, requests, tile_dst, tile_src, tile_masks, tile_count):
    count = tile_count.reshape(1, 1)
    masks = tile_masks[0]
    fara, farb, *rest = exchange(node_feats, weight, requests, att_src, att_dst, out_bias, tile_dst, tile_src, count, masks)
    fara = fara.reshape(PEERS, J, F)
    farb = farb.reshape(PEERS, J, F)
    return attend(tile_dst, tile_src, count, fara, farb, *rest, masks)


def solution(mesh):
    placed = (
        P("node", None), P(), P(), P(), P(), P("node", None), P("node", None), P("node", None),
        P("node", None, None, None), P("node"),
    )
    return jax.shard_map(local, mesh=mesh, in_specs=placed, out_specs=P("node", None), check_vma=False)
```

time: 135 us -> 202 us (1.50)
  the two profiles are of different devices: /device:TPU:7 before, /device:TPU:70 now
where the time goes in v4:
time: 202 us; the launch traced here: 199 us
  Pallas kernels  198 us (98%)
    pallas_call x1, Pallas kernels, attend(): pl.pallas_call(attend_kernel, out_shape=jax.ShapeDtypeStruct((NB * BLK, F...  155 us
    pallas_call x1, Pallas kernels, exchange(): pl.pallas_call(exchange_kernel, out_shape=(jax.ShapeDtypeStruct(far, BF),...  43.2 us

profile of v4, /device:TPU:70, one launch (start us, length us, event | category | flops | bytes accessed | tf_op | source)
XLA Modules:
  0.0 199.1 jit_solution(8087784391345507188)
XLA Ops:
  0.7 43.2 %exchange.1 = (bf16[4,4,4,2,64,128]{5,4,3,2,1,0:T(8,128)(2,1)}, bf16[4,4,4,2,64,128]{5,4,3,2,1,0:T(8,128)(2,1)}, bf16[1024,128]{1,0:T(8,128)(2,1)}, bf16[8,4,128...) custom-call(bf16[1024,128]{1,0:T(8,128)(2,1)} %x_hbm.1, ...), custom_call_target="tpu_custom_call" | custom-call | tf_op jit(solution)/shard_map/exchange/pallas_call | solution.py:720
  43.8 155.2 %attend.1 = bf16[1024,128]{1,0:T(8,128)(2,1)} custom-call(s32[1,128]{1,0:T(1,128)} %dst_hbm.3, s32[1,128]{1,0:T(1,128)} %src_hbm.3, s32[1,1]{1,0:T(1,128)} %bitcast.6.cnt_hbm, bf16[128,64,128]{2,1,0:T(8,128)(2,1)} %bitcast.9, bf16[128,64,128]{2,1,0:T(8,128)(2,1)} %bitcast.10, bf16[1024,128]{1,0:T(8,128)(2,1)} %get-tuple-element.15.own_hbm, ...), custom_call_target="tpu_custom_call" | custom-call | tf_op jit(solution)/shard_map/attend/pallas_call | solution.py:325

commit v5 on v4

--- a/solution.py
+++ b/solution.py
@@ -14,7 +14,7 @@
 NB = 8
 TILES = 128
 PEERS = 128
-GROUP = 16
+GROUP = 32
 PART = 32
 J = BLK // 2
 GROUPS = TILES // GROUP
@@ -94,7 +94,7 @@
     small = (J // ROWS, ROWS, F)
     v = v.reshape(small)
     m = m.reshape(cut)
-    sums = []
+    w_rows, v_cols = [], []
     for side in range(2):
         weights = []
         for pair in range(2):
@@ -108,9 +108,10 @@
             h = side * (HEADS // 2) + i
             mine = jnp.broadcast_to((head_id == h)[None], small)
             values.append(jnp.where(mine, v, jnp.broadcast_to(ones_ref[h][None], small)).reshape(J, F))
-        sums.append(jnp.dot(jnp.concatenate(weights, axis=1), jnp.concatenate(values, axis=0),
-                            preferred_element_type=F32))
-    return sums
+        w_rows.append(jnp.concatenate(weights, axis=1))
+        v_cols.append(jnp.concatenate(values, axis=0))
+    o = jnp.dot(jnp.concatenate(w_rows, axis=0), jnp.concatenate(v_cols, axis=1), preferred_element_type=F32)
+    return o[0:BLK, 0:F], o[BLK:2 * BLK, F:2 * F]
 
 
 def lane_marks(head_ref, ones_ref):
@@ -142,7 +143,7 @@
 
 
 def attend_body(dst_hbm, src_hbm, cnt_hbm, fara_hbm, farb_hbm, own_hbm, q_hbm, acc_hbm, par_hbm, mb_hbm, part_hbm,
-                mask_hbm, out_ref, masks, fara_ref, s_ref, b_ref, d_ref, acc, dmat, pmat, slog, own_ref, par_ref,
+                mask_hbm, out_ref, masks, fara_ref, s_ref, b_ref, d_ref, acc, self_ref, dmat, pmat, slog, own_ref, par_ref,
                 dst_ref, src_ref, cnt_ref, far_sem, in_sem, mb_sem, part_sem, late_sem,
                 q_ref, far_ref, bd_ref, m_ref, part_ref, head_ref, ones_ref):
     def far_copy(c):
@@ -158,16 +159,20 @@
         pltpu.make_async_copy(src, dst, in_sem.at[i])
         for i, (src, dst) in enumerate((
             (par_hbm, par_ref), (cnt_hbm, cnt_ref), (dst_hbm, dst_ref), (src_hbm, src_ref),
-            (q_hbm, q_ref), (acc_hbm, acc), (own_hbm, own_ref)))
+            (q_hbm, q_ref)))
     ]
     inputs[0].start()
     for c in range(PEERS // PART):
         far_copy(c).start()
     for copy in inputs[1:]:
         copy.start()
+    self_copy = pltpu.make_async_copy(acc_hbm, self_ref, late_sem.at[2])
     for g in range(GROUPS):
         for copy in group_copies(g):
             copy.start()
+        if g == 0:
+            self_copy.start()
+    acc[...] = jnp.zeros_like(acc)
     inputs[0].wait()
 
     a_s = par_ref[0:8]
@@ -213,12 +218,15 @@
 
         lax.fori_loop(0, live, group, 0)
         lax.fori_loop(live, GROUPS, group_wait, 0)
+        self_copy.wait()
 
     @pl.when(jnp.logical_not(bounded))
     def _():
         lax.fori_loop(0, GROUPS, group_wait, 0)
+        self_copy.wait()
         late = (pltpu.make_async_copy(mask_hbm, masks, late_sem.at[0]),
-                pltpu.make_async_copy(fara_hbm, fara_ref, late_sem.at[1]))
+                pltpu.make_async_copy(fara_hbm, fara_ref, late_sem.at[1]),
+                pltpu.make_async_copy(own_hbm, own_ref, late_sem.at[3]))
         for copy in late:
             copy.start()
         for copy in late:
@@ -284,7 +292,7 @@
             return 0
 
         lax.fori_loop(0, NB, settle, 0)
-        self_sums(acc, own_ref[...], slog[...])
+        self_sums(self_ref, own_ref[...], slog[...])
         lane2 = iota((J, F), 1)
 
         def tile(t, _):
@@ -307,8 +315,8 @@
 
     bias = par_ref[24:25]
     for b in range(NB):
-        one = acc[b, :, 0:F]
-        two = acc[b, :, F:2 * F]
+        one = acc[b, :, 0:F] + self_ref[b, :, 0:F]
+        two = acc[b, :, F:2 * F] + self_ref[b, :, F:2 * F]
         left = lane1 < F // 2
         top = jnp.where(left, one, two)
         low_part = pltpu.roll(jnp.where(left, two, one), F // 2, 1)
@@ -334,6 +342,7 @@
             pltpu.VMEM((PEERS, HEADS, BLK), F32),
             pltpu.VMEM((PEERS, HEADS, BLK), F32),
             pltpu.VMEM((NB, BLK, 2 * F), F32),
+            pltpu.VMEM((NB, BLK, 2 * F), F32),
             pltpu.VMEM((NB, HEADS, BLK, F), F32),
             pltpu.VMEM((NB, HEADS, BLK, F), F32),
             pltpu.VMEM((NB * BLK, F), F32),
@@ -342,7 +351,7 @@
             pltpu.SMEM((1, TILES), jnp.int32),
             pltpu.SMEM((1, TILES), jnp.int32),
             pltpu.SMEM((1, 1), jnp.int32),
-            dma((PEERS // PART,)), dma((7,)), dma((GROUPS,)), dma((GROUPS,)), dma((2,)),
+            dma((PEERS // PART,)), dma((5,)), dma((GROUPS,)), dma((GROUPS,)), dma((4,)),
         ],
         compiler_params=pltpu.CompilerParams(vmem_limit_bytes=VMEM_ALL),
         name="attend",
@@ -350,9 +359,9 @@
 
 
 SIDE = 4
-SPLIT = (("z", "y", "x"), ("x", "z", "y"), ("y", "x", "z")) * 2
-ROW_AT = (0, 24, 48, 0, 24, 48)
-SPANS = (24, 24, 16) * 2
+SPLIT = (("z", "y", "x"), ("x", "z", "y"), ("y", "x", "z"), ("y", "z", "x"), ("z", "x", "y"), ("x", "y", "z"))
+ROW_AT = (0, 24, 48, 0, 24, 40)
+SPANS = (24, 24, 16, 24, 16, 24)
 WAYS = len(SPLIT)
 EARLY = (0, 1, 2)
 LATER = (3, 4, 5)
@@ -520,8 +529,8 @@
 
     def group_gives(g):
         rows = pl.ds(g * GROUP, GROUP)
-        return (pltpu.make_async_copy(mb_ref.at[rows], mb_hbm.at[rows], mb_sem.at[g]),
-                pltpu.make_async_copy(part_ref.at[rows], part_hbm.at[rows], part_sem.at[g]))
+        return (lambda: pltpu.make_async_copy(mb_ref.at[rows], mb_hbm.at[rows], mb_sem.at[g]),
+                lambda: pltpu.make_async_copy(part_ref.at[rows], part_hbm.at[rows], part_sem.at[g]))
 
     for i in range(3):
         for c in EARLY:
@@ -572,6 +581,23 @@
     for g in gives:
         g.start()
 
+    count = cnt_ref[0, 0]
+    left = iota((BLK, BLK), 1) < J
+    lane_marks(head_ref, ones_ref)
+
+    def prepare(g, _):
+        mask_copy(g).wait()
+        for k in range(GROUP):
+            t = g * GROUP + k
+            m = masks[t].astype(F32) * (t < count).astype(F32)
+            turned = pltpu.roll(m, J, 1)
+            ma_ref[t] = jnp.where(left, m, turned).astype(BF)
+            mb_ref[t] = jnp.where(left, turned, m).astype(BF)
+        group_gives(g)[0]().start()
+        return 0
+
+    lax.fori_loop(0, GROUPS // 2, prepare, 0)
+
     def spread_second(ways):
         for k in range(1, SIDE):
             for c in ways:
@@ -580,9 +606,6 @@
                     second(c, k, i).start()
 
     spread_second(EARLY)
-    for i in range(2):
-        for c in LATER:
-            second(c, 0, i).start()
     all_asks().wait_recv()
     fetch = pltpu.make_async_copy(rq, rqs, smem_sem.at[0])
     fetch.start()
@@ -606,21 +629,6 @@
                 else:
                     picked[c][q, j, a_at] = part
 
-    count = cnt_ref[0, 0]
-    left = iota((BLK, BLK), 1) < J
-    lane_marks(head_ref, ones_ref)
-
-    def prepare(g, _):
-        mask_copy(g).wait()
-        for k in range(GROUP):
-            t = g * GROUP + k
-            m = masks[t].astype(F32) * (t < count).astype(F32)
-            turned = pltpu.roll(m, J, 1)
-            ma_ref[t] = jnp.where(left, m, turned).astype(BF)
-            mb_ref[t] = jnp.where(left, turned, m).astype(BF)
-        group_gives(g)[0].start()
-        return 0
-
     def pass_on(c, q):
         for k in range(SIDE):
             second(c, k, q - 1).wait_recv()
@@ -635,13 +643,15 @@
 
     for c in EARLY:
         hand_out(c, 0)
-    lax.fori_loop(0, GROUPS // 2, prepare, 0)
+    lax.fori_loop(GROUPS // 2, GROUPS, prepare, 0)
+    for i in range(2):
+        for c in LATER:
+            second(c, 0, i).start()
     spread_second(LATER)
     for q in (1, 2):
         for c in EARLY:
             pass_on(c, q)
             hand_out(c, q)
-    lax.fori_loop(GROUPS // 2, GROUPS, prepare, 0)
     for c in EARLY:
         all_onward(c).wait_recv()
         hand_out(c, 3)
@@ -651,10 +661,6 @@
     for q in (0, 1, 2):
         for c in LATER:
             hand_out(c, q)
-    for c in LATER:
-        all_onward(c).wait_recv()
-        hand_out(c, 3)
-
     for q in range(SIDE):
         for c in EARLY:
             all_third(c, q).wait_recv()
@@ -683,8 +689,12 @@
             sums = half_tile(k, dst_ref[0, t], q_out, v_ref[k], ma_ref[t], bd_ref, head_id, ones_ref)
             for side in range(2):
                 part_ref[t, :, side * F:(side + 1) * F] = sums[side].astype(BF)
-        group_gives(g)[1].start()
+        group_gives(g)[1]().start()
         return 0
+
+    for c in LATER:
+        all_onward(c).wait_recv()
+        hand_out(c, 3)
 
     lax.fori_loop(0, GROUPS, group, 0)
 
@@ -700,7 +710,7 @@
             bulk(gathered[c][3].at[:, pl.ds(0, NB // 2)], fwd_s.at[c, i], fwd_r.at[c]).wait_send()
     for g in range(GROUPS):
         for copy in group_gives(g):
-            copy.wait()
+            copy().wait()
     for q in range(SIDE):
         for c in range(WAYS):
             all_third(c, q).wait_send()

time: 202 us -> 199 us (0.985)
    pallas_call x1, Pallas kernels: 43.2 us -> 40.7 us  [exchange(): pl.pallas_call(exchange_kernel, out_shape=(jax.ShapeDtypeStruct(far, BF),...]
where the time goes in v5:
time: 199 us; the launch traced here: 196 us
  Pallas kernels  196 us (98%)
    pallas_call x1, Pallas kernels, attend(): pl.pallas_call(attend_kernel, out_shape=jax.ShapeDtypeStruct((NB * BLK, F...  155 us
    pallas_call x1, Pallas kernels, exchange(): pl.pallas_call(exchange_kernel, out_shape=(jax.ShapeDtypeStruct(far, BF),...  40.7 us

profile of v5, /device:TPU:70, one launch (start us, length us, event | category | flops | bytes accessed | tf_op | source)
XLA Modules:
  0.0 196.5 jit_solution(14101185256898560346)
XLA Ops:
  0.7 40.7 %exchange.1 = (bf16[4,4,4,2,64,128]{5,4,3,2,1,0:T(8,128)(2,1)}, bf16[4,4,4,2,64,128]{5,4,3,2,1,0:T(8,128)(2,1)}, bf16[1024,128]{1,0:T(8,128)(2,1)}, bf16[8,4,128...) custom-call(bf16[1024,128]{1,0:T(8,128)(2,1)} %x_hbm.1, ...), custom_call_target="tpu_custom_call" | custom-call | tf_op jit(solution)/shard_map/exchange/pallas_call | solution.py:730
  41.3 155.2 %attend.1 = bf16[1024,128]{1,0:T(8,128)(2,1)} custom-call(s32[1,128]{1,0:T(1,128)} %dst_hbm.3, s32[1,128]{1,0:T(1,128)} %src_hbm.3, s32[1,1]{1,0:T(1,128)} %bitcast.6.cnt_hbm, bf16[128,64,128]{2,1,0:T(8,128)(2,1)} %bitcast.9, bf16[128,64,128]{2,1,0:T(8,128)(2,1)} %bitcast.10, bf16[1024,128]{1,0:T(8,128)(2,1)} %get-tuple-element.15.own_hbm, ...), custom_call_target="tpu_custom_call" | custom-call | tf_op jit(solution)/shard_map/attend/pallas_call | solution.py:333
